TPU v7x, 128 devices: a whole 4x4x4 slice. The times are simulated.
128 devices in a mesh: rep: 8 (over z, y_lo), fsdp: 16 (over y_hi, x, core).
Axes of the slice: x: 4, y: 4 (y_hi: 2, y_lo: 2; y = y_hi * 2 + y_lo), z: 4, core: 2. Of those that a mesh axis runs over, the one named last changes fastest.
Arguments:
- tokens: bfloat16 [65536, 2048], P(('rep', 'fsdp')), may hold values from -6 to 6
- norm_gain: float32 [2048], replicated, may hold values from 0.5 to 1.5
- outer_params: float32 [2, 2048, 4096], P(None, 'fsdp'), may hold values from -6 to 6
- momentum: float32 [2, 2048, 4096], P(None, 'fsdp'), may hold values from -6 to 6
- deltas: bfloat16 [8, 2, 2048, 4096], P('rep', None, 'fsdp'), may hold values from -6 to 6
Outputs:
- new_params: float32 [2, 2048, 4096], P(None, 'fsdp')
- new_momentum: float32 [2, 2048, 4096], P(None, 'fsdp')
- hidden: bfloat16 [65536, 4096], P(('rep', 'fsdp'))
All inputs are finite; a program needn't handle non-finite values.
Results may differ from a plain program's by a relative error of at most 0.01.
Values may be sent and summed in bfloat16 or wider, within the bound.
A program may use at most 192 MiB of HBM per device.

v0:
```python
import math

import jax
import jax.numpy as jnp
from jax import lax
from jax.sharding import PartitionSpec as P

EPS = 1e-05
MU = 0.9
RATE = 0.7


def advance(params, moment, summed, groups):
    outer_grad = summed * (1.0 / groups)
    moment_next = MU * moment + outer_grad
    params_next = params - RATE * (outer_grad + MU * moment_next)
    return (params_next, moment_next)


def body(tokens, norm_gain, outer_params, momentum, deltas):
    groups = lax.axis_size("rep")
    own_delta = deltas[0].astype(jnp.float32)
    summed = lax.psum(own_delta.astype(jnp.bfloat16), "rep").astype(jnp.float32)
    new_params, new_momentum = advance(outer_params, momentum, summed, groups)
    weights = new_params.astype(jnp.bfloat16)
    values = tokens.astype(jnp.float32)
    scale_rows = lax.rsqrt(jnp.mean(values * values, axis=-1, keepdims=True) + EPS)
    normed = (values * scale_rows * norm_gain).astype(jnp.bfloat16)
    factor = 1.0 / math.sqrt(normed.shape[1])
    results = []
    for which in range(2):
        results.append(
            jnp.dot(
                normed,
                lax.all_gather(weights[which], "fsdp", axis=0, tiled=True),
                preferred_element_type=jnp.float32,
            )
        )
    gate, up = (results[0], results[1])
    hidden = (jax.nn.silu(gate * factor) * (up * factor)).astype(jnp.bfloat16)
    return (new_params, new_momentum, hidden)


def solution(mesh):
    in_specs = (
        P(("rep", "fsdp"), None),
        P(),
        P(None, "fsdp", None),
        P(None, "fsdp", None),
        P("rep", None, "fsdp", None),
    )
    out_specs = (P(None, "fsdp", None), P(None, "fsdp", None), P(("rep", "fsdp"), None))
    return jax.shard_map(body, mesh=mesh, in_specs=in_specs, out_specs=out_specs, check_vma=False)
```

profile of v0, /device:TPU:1, one launch (start us, length us, event | category | flops | bytes accessed | tf_op | source)
XLA Modules:
  0.0 376.3 jit_solution(11234318730406531627)
XLA Ops:
  7.2 0.0 all-reduce.2.cloned.1.call-start
  7.2 0.7 all-reduce.2.cloned.1.call-update
  7.9 0.0 all-gather.7.cloned.1.call-start
  7.9 109.9 %all-reduce.2.cloned.1.call-done = bf16[2,128,4096]{2,1,0:T(8,128)(2,1)} async-done(((bf16[2,128,4096]{2,1,0:T(8,128)(2,1)}), bf16[2,128,4096]{2,1,0:T(8,128)(2,1)}) %all-reduce.2.cloned.1.call-update) | async-done | bytes 2097168 | tf_op jit(solution)/shard_map/psum | solution.py:23
  117.9 9.4 %fusion.11 = (bf16[2,128,4096]{2,1,0:T(8,128)(2,1)S(1)}, f32[2,128,4096]{2,1,0:T(8,128)}, f32[2,128,4096]{2,1,0:T(8,128)}) fusion(f32[2,128,4096]{2,1,0:T(8,128)} %param.7, bf16[2,128,4096]{2,1,0:T(8,128)(2,1)} %all-reduce.2.cloned.1.call-done, f32[2,128,4096]{2,1,0:T(8,128)} %param.8), kind=kLoop, calls=%fused_computation.14 | loop fusion | flops 9437184 | bytes 20971520 | tf_op jit(solution)/shard_map/convert_element_type | solution.py:25
  127.3 0.0 copy-start
  127.3 0.0 copy-start.1
  127.3 1.5 fusion.12
  128.7 0.0 all-gather.7.cloned.1.call-update
  128.7 0.0 all-gather.5.cloned.1.call-start
  128.8 0.7 all-gather.5.cloned.1.call-update
  129.5 0.1 copy-done
  129.6 0.5 fusion.6
  130.1 108.7 %all-gather.7.cloned.1.call-done = bf16[1,2048,4096]{2,1,0:T(8,128)(2,1)} async-done(((bf16[1,128,4096]{2,1,0:T(8,128)(2,1)}), bf16[1,2048,4096]{2,1,0:T(8,128)(2,1)}) %all-gather.7.cloned.1.call-update) | async-done | bytes 16777232 | tf_op jit(solution)/shard_map/all_gather | solution.py:35
  238.8 0.0 copy-done.1
  238.8 14.4 %fusion = f32[512,4096]{1,0:T(8,128)} fusion(bf16[1,2048,4096]{2,1,0:T(8,128)(2,1)} %all-gather.7.cloned.1.call-done, bf16[512,2048]{1,0:T(8,128)(2,1)S(1)} %copy-done, f32[2048]{0:T(1024)S(1)} %copy-done.1, f32[512]{0:T(512)S(1)} %add_rsqrt_fusion), kind=kOutput, calls=%fused_computation | convolution fusion | flops 8594128896 | bytes 27273216 | tf_op jit(solution)/shard_map/dot_general | solution.py:33
  253.2 96.1 %all-gather.5.cloned.1.call-done = bf16[1,2048,4096]{2,1,0:T(8,128)(2,1)} async-done(((bf16[1,128,4096]{2,1,0:T(8,128)(2,1)}), bf16[1,2048,4096]{2,1,0:T(8,128)(2,1)}) %all-gather.5.cloned.1.call-update) | async-done | bytes 16777232 | tf_op jit(solution)/shard_map/all_gather | solution.py:35
  349.3 20.5 %multiply_convert_fusion = bf16[512,4096]{1,0:T(8,128)(2,1)} fusion(f32[512,4096]{1,0:T(8,128)} %fusion, bf16[1,2048,4096]{2,1,0:T(8,128)(2,1)} %all-gather.5.cloned.1.call-done, bf16[512,2048]{1,0:T(8,128)(2,1)S(1)} %copy-done, f32[2048]{0:T(1024)S(1)} %copy-done.1, f32[512]{0:T(512)S(1)} %add_rsqrt_fusion), kind=kOutput, calls=%fused_computation.4 | convolution fusion | flops 8610906112 | bytes 31467520 | tf_op jit(solution)/shard_map/dot_general | solution.py:33
  (1 shorter events, 0.0 us)
Async XLA Ops:
  7.2 110.7 %all-reduce.2.cloned.1.call-start = ((), (), s32[]{:S(2)}) async-start(), calls=%async_computation | async-start | bytes 4194304 | tf_op jit(solution)/shard_map/psum | solution.py:23
  7.9 230.9 %all-gather.7.cloned.1.call-start = ((), (), s32[]{:S(2)}) async-start(), calls=%async_computation.2 | async-start | bytes 17825792 | tf_op jit(solution)/shard_map/all_gather | solution.py:35
  127.3 2.3 copy-start
  127.3 111.6 %copy-start.1 = (f32[2048]{0:T(1024)S(1)}, f32[2048]{0:T(1024)}, u32[]{:S(2)}) copy-start(f32[2048]{0:T(1024)} %param.6) | copy-start | bytes 24580
  128.7 220.6 %all-gather.5.cloned.1.call-start = ((), (), s32[]{:S(2)}) async-start(), calls=%async_computation.1 | async-start | bytes 17825792 | tf_op jit(solution)/shard_map/all_gather | solution.py:35
Sparse Core Ops, SparseCore 0:
  10.5 107.3 all-reduce.1
  128.9 109.9 all-gather.6
  241.8 107.4 all-gather.4
where the time goes:
time: 376 us
  waiting for transfers between devices  316 us (84%)
  matrix products  34.9 us (9%)
  between operations  13.7 us (4%)
  other arithmetic  9.89 us (3%)
    all_gather x2, waiting for transfers between devices, body(): lax.all_gather(weights[which], 'fsdp', axis=0, tiled=True)  205 us
    psum x1, waiting for transfers between devices, body(): summed = lax.psum(own_delta.astype(jnp.bfloat16), 'rep').astype(jnp.float32)  110 us
    dot_general x2, matrix products, body(): jnp.dot(normed, lax.all_gather(weights[which], 'fsdp', axis=0, tiled=True...  34.9 us
    convert_element_type x1, other arithmetic, body(): weights = new_params.astype(jnp.bfloat16)  9.4 us
  transfers between devices with their start and end apart: 3, of which 3 were waited for; matrix products, arithmetic and copies ran while one was open for 4% of the time, Pallas kernels for 0%

commit v1 on v0

v1 whole, which is shorter than its diff:
```python
import functools
import math

import jax
import jax.numpy as jnp
from jax import lax
from jax.experimental import pallas as pl
from jax.experimental.pallas import tpu as pltpu
from jax.sharding import PartitionSpec as P

EPS = 1e-05
MU = 0.9
RATE = 0.7
MESH = pl.DeviceIdType.MESH
ALL = slice(None)

ORDERS = {"x": ("y", "z", "x"), "y": ("z", "x", "y"), "z": ("x", "y", "z")}
SETS = ({"x": (0, 6), "y": (6, 5), "z": (11, 5)},)
UNITS = 16
LANES = 128
HALF = 2048


def advance(params, moment, outer_grad):
    moment_next = MU * moment + outer_grad
    params_next = params - RATE * (outer_grad + MU * moment_next)
    return (params_next, moment_next)


def kernel(
    tokens, gain, params, moment, deltas, hidden, grads,
    wts, tok, normed, got, pbuf, mbuf, gsum, stage, hbuf,
    loc, rs_s, rs_r, tk_s, tk_r, dd_s, dd_r, p1_s, p1_r, p2_s, p2_r, p3_s, p3_r,
    g_s, g_r, h_l, h_s, h_r,
):
    rep = lax.axis_index("rep")
    fsdp = lax.axis_index("fsdp")
    z, yl = rep // 2, rep % 2
    yh, x, core = fsdp // 8, (fsdp // 2) % 4, fsdp % 2
    y = yh * 2 + yl
    here = {"x": x, "y": y, "z": z}

    def device(at, c):
        return (at["z"] * 2 + at["y"] % 2, (at["y"] // 2) * 8 + at["x"] * 2 + c)

    def shifted(axis, step):
        return {**here, axis: (here[axis] + step + 4) % 4}

    partner = (rep, yh * 8 + x * 2 + (1 - core))
    ydev = device({**here, "y": yh * 2 + (1 - yl)}, core)

    def rep_peer(k):
        return ((z + k // 2) % 4) * 2 + (yl + k % 2) % 2

    barrier = pltpu.get_barrier_semaphore()
    greet = [device(shifted(a, d), core) for a in "xyz" for d in (1, -1)]
    greet += [partner] + [(rep_peer(k), fsdp) for k in range(1, 8)]
    for who in greet:
        pl.semaphore_signal(barrier, inc=1, device_id=who, device_id_type=MESH)

    locals_ = [
        pltpu.make_async_copy(tokens, tok.at[0], loc.at[0]),
        pltpu.make_async_copy(deltas.at[:, rep], got.at[0], loc.at[1]),
        pltpu.make_async_copy(params.at[:, rep], pbuf, loc.at[2]),
        pltpu.make_async_copy(moment.at[:, rep], mbuf, loc.at[3]),
    ]
    for c in locals_:
        c.start()
    pl.semaphore_wait(barrier, len(greet))

    sent = []

    def remote(src, dst, s, r, who):
        return pltpu.make_async_remote_copy(
            src_ref=src, dst_ref=dst, send_sem=s, recv_sem=r, device_id=who, device_id_type=MESH
        )

    def send(src, dst, s, r, who):
        c = remote(src, dst, s, r, who)
        c.start()
        sent.append(c)

    for k in (4, 5, 2, 3, 6, 7, 1):
        q = rep_peer(k)
        send(deltas.at[:, q], got.at[k], rs_s.at[k], rs_r.at[k], (q, fsdp))
    send(tokens, tok.at[1], tk_s, tk_r, partner)

    locals_[0].wait()
    remote(tokens, tok.at[1], tk_s, tk_r, partner).wait_recv()
    chunk = 32

    def norm_step(i, carry):
        rows = pl.ds(pl.multiple_of((i % 16) * chunk, chunk), chunk)
        v = tok[i // 16, rows, :].astype(jnp.float32)
        scale = lax.rsqrt(jnp.mean(v * v, axis=-1, keepdims=True) + EPS)
        normed[pl.ds(pl.multiple_of(i * chunk, chunk), chunk), :] = (v * scale * gain[...]).astype(jnp.bfloat16)
        return carry

    lax.fori_loop(0, 1024 // chunk, norm_step, 0)

    for c in locals_[1:]:
        c.wait()
    for k in range(1, 8):
        remote(got.at[k], got.at[k], rs_s.at[k], rs_r.at[k], partner).wait_recv()

    def update_step(j, carry):
        for other in (True, False):
            col = ((1 - core) if other else core) * HALF + j * LANES
            cols = pl.ds(pl.multiple_of(col, LANES), LANES)
            for mat in range(2):
                acc = got[0, mat, :, cols].astype(jnp.float32)
                for k in range(1, 8):
                    acc = acc + got[k, mat, :, cols].astype(jnp.float32)
                g = acc * (1.0 / 8)
                gsum[mat, z, yl, :, cols] = g.astype(jnp.bfloat16)
                new, _ = advance(pbuf[mat, :, cols], mbuf[mat, :, cols], g)
                w = new.astype(jnp.bfloat16)
                lanes = pl.ds(mat * LANES, LANES)
                if other:
                    stage[j, :, lanes] = w
                else:
                    wts[j, yh, x, core, z, yl, :, lanes] = w
        return carry

    lax.fori_loop(0, UNITS, update_step, 0)
    send(stage, wts.at[:, yh, x, core, z, yl], dd_s, dd_r, partner)
    remote(stage, wts.at[:, yh, x, 1 - core, z, yl], dd_s, dd_r, partner).wait_recv()

    def region(us, at, half=ALL):
        ax, ay, az = at["x"], at["y"], at["z"]
        fx = ALL if ax is None else ax
        fz = ALL if az is None else az
        fh, fl = (ALL, ALL) if ay is None else (ay // 2, ay % 2)
        return wts.at[us, fh, fx, half, fz, fl]

    class Ring:
        def __init__(self, us, order, phase, s, r):
            self.us, self.axis, self.s, self.r = us, order[phase], s, r
            self.base = {a: (None if a in order[:phase] else here[a]) for a in "xyz"}
            self.to = [device(shifted(self.axis, d), core) for d in (1, -1)]

        def at(self, step):
            return {**self.base, self.axis: (here[self.axis] + step + 4) % 4}

        def start(self):
            own = region(self.us, self.at(0))
            for d in range(2):
                send(own, own, self.s.at[d], self.r.at[d], self.to[d])

        def forward(self):
            for d in range(2):
                back = self.at(-1 if d == 0 else 1)
                full = region(self.us, back)
                remote(full, full, self.s.at[d], self.r.at[d], self.to[d]).wait_recv()
                part = region(self.us, back, d)
                send(part, part, self.s.at[2 + d], self.r.at[2 + d], self.to[d])

        def finish(self):
            for d in range(2):
                far = region(self.us, self.at(2), d)
                remote(far, far, self.s.at[2 + d], self.r.at[2 + d], self.to[d]).wait_recv()

    names = ("x", "y", "z")
    parts = SETS[0]

    def rings(phase, s, r):
        return [
            Ring(pl.ds(parts[n][0], parts[n][1]), ORDERS[n], phase, s.at[i], r.at[i])
            for i, n in enumerate(names)
        ]

    for phase, s, r in ((0, p1_s, p1_r), (1, p2_s, p2_r)):
        group = rings(phase, s, r)
        for step in ("start", "forward", "finish"):
            for ring in group:
                getattr(ring, step)()
        if phase == 0:
            own = gsum.at[:, z, yl]
            send(own, own, g_s.at[4], g_r.at[4], ydev)

    factor = 1.0 / math.sqrt(2048)

    def compute(u):
        def rows_step(m, carry):
            w = wts[u].reshape(2048, 2 * LANES)
            rows = pl.ds(pl.multiple_of(m * 512, 512), 512)
            out = jnp.dot(normed[rows, :], w, preferred_element_type=jnp.float32)
            gate = out[:, :LANES] * factor
            up = out[:, LANES:] * factor
            hbuf[u, m] = ((gate / (1.0 + jnp.exp(-gate))) * up).astype(jnp.bfloat16)
            return carry

        lax.fori_loop(0, 2, rows_step, 0)

    def hidden_cols(c, u):
        return hidden.at[:, pl.ds(pl.multiple_of(c * HALF + u * LANES, LANES), LANES)]

    copies = []

    def emit(u):
        c = pltpu.make_async_copy(hbuf.at[u, 0], hidden_cols(core, u), h_l.at[u])
        c.start()
        copies.append(c)
        send(hbuf.at[u, 1], hidden_cols(core, u), h_s.at[u], h_r.at[u], partner)

    rounds = []
    for k in range(max(parts[n][1] for n in names)):
        us = [(n, parts[n][0] + k) for n in names if k < parts[n][1]]
        rounds.append(
            ([Ring(pl.ds(u, 1), ORDERS[n], 2, p3_s.at[u], p3_r.at[u]) for n, u in us], [u for _, u in us])
        )

    def g_region(step):
        return gsum.at[:, (z + step + 4) % 4]

    zto = [device(shifted("z", d), core) for d in (1, -1)]
    for ring in rounds[0][0]:
        ring.start()
    for k in range(len(rounds)):
        if k + 1 < len(rounds):
            for ring in rounds[k + 1][0]:
                ring.start()
        if k == 0:
            far = gsum.at[:, z, 1 - yl]
            remote(far, far, g_s.at[4], g_r.at[4], ydev).wait_recv()
            for d in range(2):
                send(g_region(0), g_region(0), g_s.at[d], g_r.at[d], zto[d])
        if k == 2:
            for d in range(2):
                back = g_region(-1 if d == 0 else 1)
                remote(back, back, g_s.at[d], g_r.at[d], zto[d]).wait_recv()
                part = gsum.at[:, (z + (3 if d == 0 else 1)) % 4, d]
                send(part, part, g_s.at[2 + d], g_r.at[2 + d], zto[d])
        for ring in rounds[k][0]:
            ring.forward()
        if k >= 1:
            for ring, u in zip(*rounds[k - 1]):
                ring.finish()
                compute(u)
            for u in rounds[k - 1][1]:
                emit(u)
    for d in range(2):
        far = gsum.at[:, (z + 2) % 4, d]
        remote(far, far, g_s.at[2 + d], g_r.at[2 + d], zto[d]).wait_recv()
    out = pltpu.make_async_copy(gsum, grads, loc.at[4])
    out.start()
    for ring, u in zip(*rounds[-1]):
        ring.finish()
        compute(u)
    for u in rounds[-1][1]:
        emit(u)
    out.wait()
    for c in copies:
        c.wait()
    for u in range(UNITS):
        remote(hbuf.at[u, 1], hidden_cols(1 - core, u), h_s.at[u], h_r.at[u], partner).wait_recv()
    for c in sent:
        c.wait_send()


def body(tokens, norm_gain, outer_params, momentum, deltas):
    bf16, f32 = jnp.bfloat16, jnp.float32
    hbm = pl.BlockSpec(memory_space=pl.ANY)
    dma = pltpu.SemaphoreType.DMA
    vmem = pltpu.VMEM
    hidden, grads = pl.pallas_call(
        kernel,
        out_shape=(
            jax.ShapeDtypeStruct((512, 4096), bf16),
            jax.ShapeDtypeStruct((2, 4, 2, 16, 4096), bf16),
        ),
        in_specs=[hbm, pl.BlockSpec(memory_space=pltpu.VMEM), hbm, hbm, hbm],
        out_specs=(hbm, hbm),
        scratch_shapes=[
            vmem((UNITS, 2, 4, 2, 4, 2, 16, 2 * LANES), bf16),
            vmem((2, 512, 2048), bf16),
            vmem((1024, 2048), bf16),
            vmem((8, 2, 16, 4096), bf16),
            vmem((2, 16, 4096), f32),
            vmem((2, 16, 4096), f32),
            vmem((2, 4, 2, 16, 4096), bf16),
            vmem((UNITS, 16, 2 * LANES), bf16),
            vmem((UNITS, 2, 512, LANES), bf16),
            dma((5,)),
            dma((8,)), dma((8,)),
            dma, dma,
            dma, dma,
            dma((3, 4)), dma((3, 4)),
            dma((3, 4)), dma((3, 4)),
            dma((UNITS, 4)), dma((UNITS, 4)),
            dma((5,)), dma((5,)),
            dma((UNITS,)), dma((UNITS,)), dma((UNITS,)),
        ],
        compiler_params=pltpu.CompilerParams(
            collective_id=0, has_side_effects=True, vmem_limit_bytes=62 * 1024 * 1024
        ),
        name="outer_round",
    )(
        tokens,
        norm_gain.reshape(1, 2048),
        outer_params.reshape(2, 8, 16, 4096),
        momentum.reshape(2, 8, 16, 4096),
        deltas.reshape(2, 8, 16, 4096),
    )
    outer_grad = grads.reshape(2, 128, 4096).astype(f32)
    new_params, new_momentum = advance(outer_params, momentum, outer_grad)
    return (new_params, new_momentum, hidden)


def solution(mesh):
    in_specs = (
        P(("rep", "fsdp"), None),
        P(),
        P(None, "fsdp", None),
        P(None, "fsdp", None),
        P("rep", None, "fsdp", None),
    )
    out_specs = (P(None, "fsdp", None), P(None, "fsdp", None), P(("rep", "fsdp"), None))
    return jax.shard_map(body, mesh=mesh, in_specs=in_specs, out_specs=out_specs, check_vma=False)
```

time: 376 us -> 146 us (0.39)
  waiting for transfers between devices: 316 us -> 0 us
  Pallas kernels: 0 us -> 134 us
  matrix products: 34.9 us -> 0 us
  between operations: 13.7 us -> 0.65 us
    all_gather x2 -> x0, waiting for transfers between devices: 205 us -> none  [body(): lax.all_gather(weights[which], 'fsdp', axis=0, tiled=True)]
    pallas_call x0 -> x1, Pallas kernels: none -> 134 us  [body(): pl.pallas_call(kernel, out_shape=(jax.ShapeDtypeStruct((512, 4096), bf16)...]
    psum x1 -> x0, waiting for transfers between devices: 110 us -> none  [body(): summed = lax.psum(own_delta.astype(jnp.bfloat16), 'rep').astype(jnp.float32)]
    dot_general x2 -> x0, matrix products: 34.9 us -> none  [body(): jnp.dot(normed, lax.all_gather(weights[which], 'fsdp', axis=0, tiled=True...]
    sub x0 -> x1, other arithmetic: none -> 9.45 us  [advance(): params_next = params - RATE * (outer_grad + MU * moment_next)]
    convert_element_type x1 -> x0, other arithmetic: 9.4 us -> none  [body(): weights = new_params.astype(jnp.bfloat16)]
  transfers between devices with their start and end apart: 3 -> 0, of which waited for: 3 -> 0; matrix products, arithmetic and copies ran while one was open for 4% -> 0% of each run, Pallas kernels for 0% -> 0%
where the time goes in v1:
time: 146 us
  Pallas kernels  134 us (92%)
  other arithmetic  9.45 us (6%)
  local copies, waits for them, and re-layouts  2.02 us (1%)
    pallas_call x1, Pallas kernels, body(): pl.pallas_call(kernel, out_shape=(jax.ShapeDtypeStruct((512, 4096), bf16)...  134 us
    sub x1, other arithmetic, advance(): params_next = params - RATE * (outer_grad + MU * moment_next)  9.45 us

profile of v1, /device:TPU:1, one launch (start us, length us, event | category | flops | bytes accessed | tf_op | source)
XLA Modules:
  0.0 145.9 jit_solution(13569304374953836152)
XLA Ops:
  0.6 133.8 %outer_round.1 = (bf16[512,4096]{1,0:T(8,128)(2,1)}, bf16[2,4,2,16,4096]{4,3,2,1,0:T(8,128)(2,1)}) custom-call(bf16[512,2048]{1,0:T(8,128)(2,1)} %tokens.1, f32[1,2048]{1,0:T(1,128)} %bitcast.12, f32[2,8,16,4096]{3,2,1,0:T(8,128)} %bitcast.9, f32[2,8,16,4096]{3,2,1,0:T(8,128)} %bitcast.10, bf16[2,8,16,4096]{3,2,1,0:T(8,128)(2,1)} %bitcast.11), custom_call_target="tpu_custom_call" | custom-call | tf_op jit(solution)/shard_map/outer_round/pallas_call | solution.py:266
  134.4 0.0 copy-start
  134.4 9.4 %fusion.1 = (f32[2,128,4096]{2,1,0:T(8,128)}, f32[2,128,4096]{2,1,0:T(8,128)}) fusion(f32[2,128,4096]{2,1,0:T(8,128)} %param.7, bf16[2,4,2,16,4096]{4,3,2,1,0:T(8,128)(2,1)} %get-tuple-element.5, f32[2,128,4096]{2,1,0:T(8,128)} %param.8), kind=kLoop, calls=%fused_computation.3 | loop fusion | flops 7340032 | bytes 18874368 | tf_op jit(solution)/shard_map/sub | solution.py:26
  143.9 0.0 copy-done
  143.9 2.0 %copy.9 = bf16[512,4096]{1,0:T(8,128)(2,1)} copy(bf16[512,4096]{1,0:T(8,128)(2,1)S(1)} %copy-done) | data formatting | bytes 8388608
Async XLA Ops:
  134.4 9.5 %copy-start = (bf16[512,4096]{1,0:T(8,128)(2,1)S(1)}, bf16[512,4096]{1,0:T(8,128)(2,1)}, u32[]{:S(2)}) copy-start(bf16[512,4096]{1,0:T(8,128)(2,1)} %get-tuple-element.14) | copy-start | bytes 12582916

commit v2 on v0

v2 whole, which is shorter than its diff:
```python
import math

import jax
import jax.numpy as jnp
from jax import lax
from jax.experimental import pallas as pl
from jax.experimental.pallas import tpu as pltpu
from jax.sharding import PartitionSpec as P

EPS = 1e-05
MU = 0.9
RATE = 0.7
MESH = pl.DeviceIdType.MESH
ALL = slice(None)
UNITS = 16
LANES = 128
HALF = 2048

ORDERS = {'x': ('y', 'z', 'x'), 'y': ('z', 'x', 'y'), 'z': ('x', 'y', 'z'), 'g': ('z', 'z', 'z', 'z')}
SPANS = ((0, 4), (4, 5), (9, 2), (11, 5))
PIECES = 2
NORMS = 4
PLAN = (
    ('rs', 0), ('rs', 1), ('norm', 0), ('norm', 1),
    ('norm', 2), ('norm', 3), ('rs2', 0), ('rs', 2),
    ('rs2', 1), ('rs', 3), ('upd', 0), ('rs2', 2),
    ('dd', 0), ('st', 0, 'z', 2, 2), ('st', 0, 'x', 0, 2), ('upd', 1),
    ('fw', 0, 'z', 2, 2), ('dd', 1), ('st', 0, 'z', 8, 1), ('st', 0, 'x', 4, 2),
    ('st', 0, 'y', 6, 2), ('fw', 0, 'x', 0, 2), ('rs2', 3), ('upd', 2),
    ('fi', 0, 'z', 2, 2), ('st', 1, 'z', 2, 1), ('st', 1, 'z', 3, 1), ('fw', 0, 'z', 8, 1),
    ('fw', 0, 'y', 6, 2), ('fw', 0, 'x', 4, 2), ('fi', 0, 'x', 0, 2), ('st', 1, 'x', 0, 1),
    ('st', 1, 'x', 1, 1), ('dd', 2), ('st', 0, 'y', 9, 2), ('fi', 0, 'z', 8, 1),
    ('st', 1, 'z', 8, 1), ('upd', 3), ('gy0',), ('fi', 0, 'y', 6, 2),
    ('st', 1, 'y', 6, 1), ('st', 1, 'y', 7, 1), ('fw', 1, 'x', 0, 1), ('fi', 0, 'x', 4, 2),
    ('st', 1, 'x', 4, 1), ('st', 1, 'x', 5, 1), ('dd', 3), ('st', 0, 'z', 15, 1),
    ('st', 0, 'y', 13, 2), ('fw', 1, 'x', 1, 1), ('fw', 1, 'z', 2, 1), ('fw', 0, 'y', 9, 2),
    ('fw', 1, 'y', 6, 1), ('fw', 1, 'z', 3, 1), ('fi', 1, 'x', 0, 1), ('st', 2, 'x', 0, 1),
    ('fw', 1, 'z', 8, 1), ('st', 0, 'x', 11, 2), ('fw', 1, 'x', 4, 1), ('fi', 1, 'y', 6, 1),
    ('fw', 0, 'z', 15, 1), ('fw', 1, 'y', 7, 1), ('st', 2, 'y', 6, 1), ('fw', 1, 'x', 5, 1),
    ('fw', 0, 'y', 13, 2), ('fi', 1, 'x', 1, 1), ('st', 2, 'x', 1, 1), ('fi', 0, 'y', 9, 2),
    ('gy1',), ('st', 3, 'g', 0, 1), ('fi', 1, 'x', 4, 1), ('fi', 1, 'z', 2, 1),
    ('fi', 1, 'x', 5, 1), ('fi', 1, 'z', 3, 1), ('fi', 0, 'y', 13, 2), ('fi', 1, 'z', 8, 1),
    ('st', 2, 'z', 2, 1), ('fw', 0, 'x', 11, 2), ('fi', 0, 'z', 15, 1), ('st', 1, 'z', 15, 1),
    ('fi', 1, 'y', 7, 1), ('st', 1, 'y', 9, 1), ('st', 2, 'y', 7, 1), ('st', 1, 'y', 10, 1),
    ('st', 1, 'y', 13, 1), ('st', 2, 'z', 3, 1), ('st', 1, 'y', 14, 1), ('fi', 0, 'x', 11, 2),
    ('fw', 2, 'x', 0, 1), ('fw', 2, 'y', 6, 1), ('fw', 1, 'y', 9, 1), ('fw', 1, 'z', 15, 1),
    ('fw', 1, 'y', 10, 1), ('st', 1, 'x', 11, 1), ('fw', 1, 'y', 13, 1), ('fw', 1, 'y', 14, 1),
    ('fw', 2, 'x', 1, 1), ('st', 1, 'x', 12, 1), ('fw', 2, 'y', 7, 1), ('fw', 2, 'z', 2, 1),
    ('fi', 2, 'x', 0, 1), ('st', 2, 'x', 4, 1), ('mm', 0), ('em', 0),
    ('st', 2, 'z', 8, 1), ('fi', 1, 'z', 15, 1), ('fi', 1, 'y', 9, 1), ('st', 2, 'y', 9, 1),
    ('fi', 1, 'y', 10, 1), ('fi', 2, 'y', 6, 1), ('fi', 1, 'y', 13, 1), ('mm', 6),
    ('em', 6), ('st', 2, 'y', 10, 1), ('fi', 1, 'y', 14, 1), ('fi', 2, 'y', 7, 1),
    ('mm', 7), ('em', 7), ('st', 2, 'x', 5, 1), ('fi', 2, 'x', 1, 1),
    ('mm', 1), ('em', 1), ('fw', 1, 'x', 11, 1), ('fw', 1, 'x', 12, 1),
    ('fi', 2, 'z', 2, 1), ('mm', 2), ('em', 2), ('fw', 2, 'z', 3, 1),
    ('fw', 2, 'y', 9, 1), ('fw', 2, 'x', 4, 1), ('st', 2, 'z', 15, 1), ('st', 2, 'y', 13, 1),
    ('fi', 1, 'x', 11, 1), ('fi', 1, 'x', 12, 1), ('st', 2, 'x', 11, 1), ('fi', 2, 'z', 3, 1),
    ('fw', 2, 'z', 8, 1), ('mm', 3), ('em', 3), ('fw', 2, 'y', 10, 1),
    ('fi', 2, 'y', 9, 1), ('mm', 9), ('em', 9), ('fw', 2, 'x', 5, 1),
    ('fw', 3, 'g', 0, 1), ('fi', 2, 'x', 4, 1), ('mm', 4), ('em', 4),
    ('st', 2, 'y', 14, 1), ('fw', 2, 'z', 15, 1), ('st', 2, 'x', 12, 1), ('fi', 2, 'z', 8, 1),
    ('st', 3, 'g', 1, 1), ('mm', 8), ('em', 8), ('fw', 2, 'y', 13, 1),
    ('fi', 2, 'y', 10, 1), ('mm', 10), ('em', 10), ('fw', 2, 'x', 11, 1),
    ('fi', 3, 'g', 0, 1), ('fi', 2, 'x', 5, 1), ('mm', 5), ('em', 5),
    ('fi', 2, 'z', 15, 1), ('mm', 15), ('em', 15), ('fw', 2, 'y', 14, 1),
    ('fw', 2, 'x', 12, 1), ('fi', 2, 'y', 13, 1), ('mm', 13), ('em', 13),
    ('fw', 3, 'g', 1, 1), ('fi', 2, 'x', 11, 1), ('mm', 11), ('em', 11),
    ('fi', 2, 'y', 14, 1), ('mm', 14), ('em', 14), ('fi', 2, 'x', 12, 1),
    ('mm', 12), ('em', 12), ('fi', 3, 'g', 1, 1),
)


def advance(params, moment, outer_grad):
    moment_next = MU * moment + outer_grad
    params_next = params - RATE * (outer_grad + MU * moment_next)
    return (params_next, moment_next)


def kernel(
    tokens, gain, params, moment, deltas, hidden, grads,
    wts, tok, normed, own0, own1, ry0, rz0, rz1, ry1, pz0, pz1, pbuf, mbuf, gsum, stage, hbuf,
    loc, a_s, a_r, b_s, b_r, tk_s, tk_r, dd_s, dd_r, ring_s, ring_r, gy_s, gy_r, h_l, h_s, h_r,
):
    bf16, f32 = jnp.bfloat16, jnp.float32
    rep = lax.axis_index("rep")
    fsdp = lax.axis_index("fsdp")
    z, yl = rep // 2, rep % 2
    yh, x, core = fsdp // 8, (fsdp // 2) % 4, fsdp % 2
    here = {"x": x, "y": yh * 2 + yl, "z": z}

    def device(at):
        return (at["z"] * 2 + at["y"] % 2, (at["y"] // 2) * 8 + at["x"] * 2 + core)

    def shifted(axis, step):
        return {**here, axis: (here[axis] + step + 4) % 4}

    partner = (rep, yh * 8 + x * 2 + (1 - core))
    ydev = (z * 2 + (1 - yl), fsdp)

    def zpos(dz):
        return (z + dz) % 4

    def zdev(dz):
        return (zpos(dz) * 2 + yl, fsdp)

    barrier = pltpu.get_barrier_semaphore()
    greet = [device(shifted(a, d)) for a in "xyz" for d in (1, -1)] + [zdev(2), partner]
    for who in greet:
        pl.semaphore_signal(barrier, inc=1, device_id=who, device_id_type=MESH)
    loads = [
        pltpu.make_async_copy(tokens, tok.at[0], loc.at[0]),
        pltpu.make_async_copy(deltas.at[0, :, yl], own0, loc.at[1]),
        pltpu.make_async_copy(deltas.at[1, z], own1, loc.at[2]),
        pltpu.make_async_copy(params.at[:, rep], pbuf, loc.at[3]),
        pltpu.make_async_copy(moment.at[:, rep], mbuf, loc.at[4]),
    ]
    for c in loads:
        c.start()
    pl.semaphore_wait(barrier, len(greet))

    sent = []

    def remote(src, dst, s, r, who):
        return pltpu.make_async_remote_copy(
            src_ref=src, dst_ref=dst, send_sem=s, recv_sem=r, device_id=who, device_id_type=MESH
        )

    def send(src, dst, s, r, who):
        c = remote(src, dst, s, r, who)
        c.start()
        sent.append(c)

    def landed(dst, s, r, who):
        remote(dst, dst, s, r, who).wait_recv()

    def lanes_at(half, first, count):
        return pl.ds(pl.multiple_of(half * HALF + first * LANES, LANES), count * LANES)

    def first_hop(s):
        out = []
        for h in range(2):
            cols = lanes_at(h, *SPANS[s])
            for dz in (2, 1, 3):
                out.append((deltas.at[1, zpos(dz), :, :, cols], rz1.at[dz - 1, :, :, cols], (s, h, dz), zdev(dz)))
            out.append((deltas.at[0, :, 1 - yl, :, cols], ry0.at[:, :, cols], (s, h, 0), ydev))
        return out

    def second_hop(s):
        out = []
        for h in range(2):
            cols = lanes_at(h, *SPANS[s])
            for dz in (2, 1, 3):
                out.append((pz0.at[dz - 1, :, cols], rz0.at[dz - 1, :, cols], (s, h, dz), zdev(dz)))
            out.append((pz1.at[:, cols], ry1.at[:, cols], (s, h, 0), ydev))
        return out

    def do_rs(s):
        for src, dst, i, who in first_hop(s):
            send(src, dst, a_s.at[i], a_r.at[i], who)
        if s == 0:
            send(tokens, tok.at[1], tk_s, tk_r, partner)

    def each_block(s, work):
        first, count = SPANS[s]

        def step(j, carry):
            work(j + first)
            return carry

        lax.fori_loop(0, count, step, 0)

    def do_rs2(s):
        if s == 0:
            for c in loads[1:]:
                c.wait()
        for _, dst, i, who in first_hop(s):
            landed(dst, a_s.at[i], a_r.at[i], who)

        def work(j):
            for h in range(2):
                cols = lanes_at(h, j, 1)
                for dz in (1, 2, 3):
                    v = own0[zpos(dz), :, cols].astype(f32) + ry0[zpos(dz), :, cols].astype(f32)
                    pz0[dz - 1, :, cols] = v.astype(bf16)
                v = own1[1 - yl, :, cols].astype(f32)
                for k in range(3):
                    v = v + rz1[k, 1 - yl, :, cols].astype(f32)
                pz1[:, cols] = v.astype(bf16)

        each_block(s, work)
        for src, dst, i, who in second_hop(s):
            send(src, dst, b_s.at[i], b_r.at[i], who)

    def do_upd(s):
        for _, dst, i, who in second_hop(s):
            landed(dst, b_s.at[i], b_r.at[i], who)

        def work(j):
            for other in (True, False):
                cols = lanes_at((1 - core) if other else core, j, 1)
                for mat in range(2):
                    if mat == 0:
                        v = own0[z, :, cols].astype(f32) + ry0[z, :, cols].astype(f32)
                        for k in range(3):
                            v = v + rz0[k, :, cols].astype(f32)
                    else:
                        v = own1[yl, :, cols].astype(f32)
                        for k in range(3):
                            v = v + rz1[k, yl, :, cols].astype(f32)
                        v = v + ry1[:, cols].astype(f32)
                    g = v * (1.0 / 8)
                    gsum[mat, z, yl, :, cols] = g.astype(bf16)
                    new, _ = advance(pbuf[mat, :, cols], mbuf[mat, :, cols], g)
                    lanes = pl.ds(mat * LANES, LANES)
                    if other:
                        stage[j, :, lanes] = new.astype(bf16)
                    else:
                        wts[j, yh, x, core, z, yl, :, lanes] = new.astype(bf16)

        each_block(s, work)
        us = pl.ds(*SPANS[s])
        send(stage.at[us], wts.at[us, yh, x, core, z, yl], dd_s.at[s], dd_r.at[s], partner)

    def do_dd(s):
        landed(wts.at[pl.ds(*SPANS[s]), yh, x, 1 - core, z, yl], dd_s.at[s], dd_r.at[s], partner)

    def region(us, at, half=ALL):
        fx = ALL if at["x"] is None else at["x"]
        fz = ALL if at["z"] is None else at["z"]
        fh, fl = (ALL, ALL) if at["y"] is None else (at["y"] // 2, at["y"] % 2)
        return wts.at[us, fh, fx, half, fz, fl]

    def ring(phase, part, first, count):
        order = ORDERS[part]
        axis = order[phase]
        row = phase * UNITS + first
        to = [device(shifted(axis, d)) for d in (1, -1)]

        def block(step, half=ALL):
            if part == "g":
                width = 2 * HALF * 2 // PIECES
                cols = pl.ds((first // 2) * width, width)
                return gsum.at[first % 2, (z + step + 4) % 4, half, :, cols]
            at = {a: (None if a in order[:phase] else here[a]) for a in "xyz"}
            return region(pl.ds(first, count), {**at, axis: (here[axis] + step + 4) % 4}, half)

        def sems(i):
            return (ring_s.at[row, i], ring_r.at[row, i], to[i % 2])

        return block, sems

    def do_st(*what):
        block, sems = ring(*what)
        for d in range(2):
            send(block(0), block(0), *sems(d))

    def do_fw(*what):
        block, sems = ring(*what)
        for d in range(2):
            back = -1 if d == 0 else 1
            landed(block(back), *sems(d))
            send(block(back, d), block(back, d), *sems(2 + d))

    def do_fi(*what):
        block, sems = ring(*what)
        for d in range(2):
            landed(block(2, d), *sems(2 + d))

    def do_gy0():
        own = gsum.at[:, z, yl]
        send(own, own, gy_s, gy_r, ydev)

    def do_gy1():
        landed(gsum.at[:, z, 1 - yl], gy_s, gy_r, ydev)

    waited = []

    def do_norm(part):
        count = 1024 // NORMS
        if not waited:
            loads[0].wait()
            waited.append(0)
        if len(waited) == 1 and (part + 1) * count > 512:
            landed(tok.at[1], tk_s, tk_r, partner)
            waited.append(1)
        chunk = 32

        def step(i, carry):
            i = i + part * (count // chunk)
            rows = pl.ds(pl.multiple_of((i % 16) * chunk, chunk), chunk)
            v = tok[i // 16, rows, :].astype(f32)
            scale = lax.rsqrt(jnp.mean(v * v, axis=-1, keepdims=True) + EPS)
            normed[pl.ds(pl.multiple_of(i * chunk, chunk), chunk), :] = (v * scale * gain[...]).astype(bf16)
            return carry

        lax.fori_loop(0, count // chunk, step, 0)

    factor = 1.0 / math.sqrt(2048)

    def do_mm(u):
        def step(m, carry):
            rows = pl.ds(pl.multiple_of(m * 512, 512), 512)
            w = wts[u].reshape(2048, 2 * LANES)
            out = jnp.dot(normed[rows, :], w, preferred_element_type=f32)
            gate = out[:, :LANES] * factor
            up = out[:, LANES:] * factor
            hbuf[u, m] = ((gate / (1.0 + jnp.exp(-gate))) * up).astype(bf16)
            return carry

        lax.fori_loop(0, 2, step, 0)

    copies = []

    def hidden_cols(c, u):
        return hidden.at[:, lanes_at(c, u, 1)]

    def do_em(u):
        c = pltpu.make_async_copy(hbuf.at[u, 0], hidden_cols(core, u), h_l.at[u])
        c.start()
        copies.append(c)
        send(hbuf.at[u, 1], hidden_cols(core, u), h_s.at[u], h_r.at[u], partner)

    does = {
        "rs": do_rs, "rs2": do_rs2, "upd": do_upd, "dd": do_dd, "st": do_st, "fw": do_fw, "fi": do_fi,
        "gy0": do_gy0, "gy1": do_gy1, "norm": do_norm, "mm": do_mm, "em": do_em,
    }
    ends = [i for i, op in enumerate(PLAN) if op[0] == "fi" and op[2] == "g"]
    for i, op in enumerate(PLAN):
        does[op[0]](*op[1:])
        if i == ends[-1]:
            c = pltpu.make_async_copy(gsum, grads, loc.at[5])
            c.start()
            copies.append(c)

    for c in copies:
        c.wait()
    for u in range(UNITS):
        landed(hidden_cols(1 - core, u), h_s.at[u], h_r.at[u], partner)
    for c in sent:
        c.wait_send()


def body(tokens, norm_gain, outer_params, momentum, deltas):
    bf16, f32 = jnp.bfloat16, jnp.float32
    hbm = pl.BlockSpec(memory_space=pl.ANY)
    dma = pltpu.SemaphoreType.DMA
    vmem = pltpu.VMEM
    spans = len(SPANS)
    hidden, grads = pl.pallas_call(
        kernel,
        out_shape=(
            jax.ShapeDtypeStruct((512, 4096), bf16),
            jax.ShapeDtypeStruct((2, 4, 2, 16, 4096), bf16),
        ),
        in_specs=[hbm, pl.BlockSpec(memory_space=pltpu.VMEM), hbm, hbm, hbm],
        out_specs=(hbm, hbm),
        scratch_shapes=[
            vmem((UNITS, 2, 4, 2, 4, 2, 16, 2 * LANES), bf16),
            vmem((2, 512, 2048), bf16),
            vmem((1024, 2048), bf16),
            vmem((4, 16, 4096), bf16),
            vmem((2, 16, 4096), bf16),
            vmem((4, 16, 4096), bf16),
            vmem((3, 16, 4096), bf16),
            vmem((3, 2, 16, 4096), bf16),
            vmem((16, 4096), bf16),
            vmem((3, 16, 4096), bf16),
            vmem((16, 4096), bf16),
            vmem((2, 16, 4096), f32),
            vmem((2, 16, 4096), f32),
            vmem((2, 4, 2, 16, 4096), bf16),
            vmem((UNITS, 16, 2 * LANES), bf16),
            vmem((UNITS, 2, 512, LANES), bf16),
            dma((6,)),
            dma((spans, 2, 4)), dma((spans, 2, 4)),
            dma((spans, 2, 4)), dma((spans, 2, 4)),
            dma, dma,
            dma((spans,)), dma((spans,)),
            dma((3 * UNITS + PIECES, 4)), dma((3 * UNITS + PIECES, 4)),
            dma, dma,
            dma((UNITS,)), dma((UNITS,)), dma((UNITS,)),
        ],
        compiler_params=pltpu.CompilerParams(
            collective_id=0, has_side_effects=True, vmem_limit_bytes=62 * 1024 * 1024
        ),
        name="outer_round",
    )(
        tokens,
        norm_gain.reshape(1, 2048),
        outer_params.reshape(2, 8, 16, 4096),
        momentum.reshape(2, 8, 16, 4096),
        deltas.reshape(2, 4, 2, 16, 4096),
    )
    outer_grad = grads.reshape(2, 128, 4096).astype(f32)
    new_params, new_momentum = advance(outer_params, momentum, outer_grad)
    return (new_params, new_momentum, hidden)


def solution(mesh):
    in_specs = (
        P(("rep", "fsdp"), None),
        P(),
        P(None, "fsdp", None),
        P(None, "fsdp", None),
        P("rep", None, "fsdp", None),
    )
    out_specs = (P(None, "fsdp", None), P(None, "fsdp", None), P(("rep", "fsdp"), None))
    return jax.shard_map(body, mesh=mesh, in_specs=in_specs, out_specs=out_specs, check_vma=False)
```

time: 376 us -> 119 us (0.32)
  waiting for transfers between devices: 316 us -> 0 us
  Pallas kernels: 0 us -> 107 us
  matrix products: 34.9 us -> 0 us
  between operations: 13.7 us -> 0.65 us
    all_gather x2 -> x0, waiting for transfers between devices: 205 us -> none  [body(): lax.all_gather(weights[which], 'fsdp', axis=0, tiled=True)]
    psum x1 -> x0, waiting for transfers between devices: 110 us -> none  [body(): summed = lax.psum(own_delta.astype(jnp.bfloat16), 'rep').astype(jnp.float32)]
    pallas_call x0 -> x1, Pallas kernels: none -> 107 us  [body(): pl.pallas_call(kernel, out_shape=(jax.ShapeDtypeStruct((512, 4096), bf16)...]
    dot_general x2 -> x0, matrix products: 34.9 us -> none  [body(): jnp.dot(normed, lax.all_gather(weights[which], 'fsdp', axis=0, tiled=True...]
    sub x0 -> x1, other arithmetic: none -> 9.45 us  [advance(): params_next = params - RATE * (outer_grad + MU * moment_next)]
    convert_element_type x1 -> x0, other arithmetic: 9.4 us -> none  [body(): weights = new_params.astype(jnp.bfloat16)]
  transfers between devices with their start and end apart: 3 -> 0, of which waited for: 3 -> 0; matrix products, arithmetic and copies ran while one was open for 4% -> 0% of each run, Pallas kernels for 0% -> 0%
where the time goes in v2:
time: 119 us
  Pallas kernels  107 us (90%)
  other arithmetic  9.45 us (8%)
  local copies, waits for them, and re-layouts  2.02 us (2%)
    pallas_call x1, Pallas kernels, body(): pl.pallas_call(kernel, out_shape=(jax.ShapeDtypeStruct((512, 4096), bf16)...  107 us
    sub x1, other arithmetic, advance(): params_next = params - RATE * (outer_grad + MU * moment_next)  9.45 us

profile of v2, /device:TPU:1, one launch (start us, length us, event | category | flops | bytes accessed | tf_op | source)
XLA Modules:
  0.0 119.3 jit_solution(3653578466882196384)
XLA Ops:
  0.6 107.2 %outer_round.1 = (bf16[512,4096]{1,0:T(8,128)(2,1)}, bf16[2,4,2,16,4096]{4,3,2,1,0:T(8,128)(2,1)}) custom-call(bf16[512,2048]{1,0:T(8,128)(2,1)} %tokens.1, f32[1,2048]{1,0:T(1,128)} %bitcast.12, f32[2,8,16,4096]{3,2,1,0:T(8,128)} %bitcast.9, f32[2,8,16,4096]{3,2,1,0:T(8,128)} %bitcast.10, bf16[2,4,2,16,4096]{4,3,2,1,0:T(8,128)(2,1)} %bitcast.11), custom_call_target="tpu_custom_call" | custom-call | tf_op jit(solution)/shard_map/outer_round/pallas_call | solution.py:349
  107.8 0.0 copy-start
  107.9 9.4 %fusion.1 = (f32[2,128,4096]{2,1,0:T(8,128)}, f32[2,128,4096]{2,1,0:T(8,128)}) fusion(f32[2,128,4096]{2,1,0:T(8,128)} %param.7, bf16[2,4,2,16,4096]{4,3,2,1,0:T(8,128)(2,1)} %get-tuple-element.5, f32[2,128,4096]{2,1,0:T(8,128)} %param.8), kind=kLoop, calls=%fused_computation.3 | loop fusion | flops 7340032 | bytes 18874368 | tf_op jit(solution)/shard_map/sub | solution.py:75
  117.3 0.0 copy-done
  117.3 2.0 %copy.9 = bf16[512,4096]{1,0:T(8,128)(2,1)} copy(bf16[512,4096]{1,0:T(8,128)(2,1)S(1)} %copy-done) | data formatting | bytes 8388608
Async XLA Ops:
  107.8 9.5 %copy-start = (bf16[512,4096]{1,0:T(8,128)(2,1)S(1)}, bf16[512,4096]{1,0:T(8,128)(2,1)}, u32[]{:S(2)}) copy-start(bf16[512,4096]{1,0:T(8,128)(2,1)} %get-tuple-element.14) | copy-start | bytes 12582916

commit v3 on v2

--- a/solution.py
+++ b/solution.py
@@ -17,56 +17,55 @@
 HALF = 2048
 
 ORDERS = {'x': ('y', 'z', 'x'), 'y': ('z', 'x', 'y'), 'z': ('x', 'y', 'z'), 'g': ('z', 'z', 'z', 'z')}
-SPANS = ((0, 4), (4, 5), (9, 2), (11, 5))
+SPANS = ((0, 5), (5, 5), (10, 2), (12, 4))
 PIECES = 2
 NORMS = 4
+SKEWED = (1, 5, 6, 13)
 PLAN = (
-    ('rs', 0), ('rs', 1), ('norm', 0), ('norm', 1),
-    ('norm', 2), ('norm', 3), ('rs2', 0), ('rs', 2),
-    ('rs2', 1), ('rs', 3), ('upd', 0), ('rs2', 2),
-    ('dd', 0), ('st', 0, 'z', 2, 2), ('st', 0, 'x', 0, 2), ('upd', 1),
-    ('fw', 0, 'z', 2, 2), ('dd', 1), ('st', 0, 'z', 8, 1), ('st', 0, 'x', 4, 2),
-    ('st', 0, 'y', 6, 2), ('fw', 0, 'x', 0, 2), ('rs2', 3), ('upd', 2),
-    ('fi', 0, 'z', 2, 2), ('st', 1, 'z', 2, 1), ('st', 1, 'z', 3, 1), ('fw', 0, 'z', 8, 1),
-    ('fw', 0, 'y', 6, 2), ('fw', 0, 'x', 4, 2), ('fi', 0, 'x', 0, 2), ('st', 1, 'x', 0, 1),
-    ('st', 1, 'x', 1, 1), ('dd', 2), ('st', 0, 'y', 9, 2), ('fi', 0, 'z', 8, 1),
-    ('st', 1, 'z', 8, 1), ('upd', 3), ('gy0',), ('fi', 0, 'y', 6, 2),
-    ('st', 1, 'y', 6, 1), ('st', 1, 'y', 7, 1), ('fw', 1, 'x', 0, 1), ('fi', 0, 'x', 4, 2),
-    ('st', 1, 'x', 4, 1), ('st', 1, 'x', 5, 1), ('dd', 3), ('st', 0, 'z', 15, 1),
-    ('st', 0, 'y', 13, 2), ('fw', 1, 'x', 1, 1), ('fw', 1, 'z', 2, 1), ('fw', 0, 'y', 9, 2),
-    ('fw', 1, 'y', 6, 1), ('fw', 1, 'z', 3, 1), ('fi', 1, 'x', 0, 1), ('st', 2, 'x', 0, 1),
-    ('fw', 1, 'z', 8, 1), ('st', 0, 'x', 11, 2), ('fw', 1, 'x', 4, 1), ('fi', 1, 'y', 6, 1),
-    ('fw', 0, 'z', 15, 1), ('fw', 1, 'y', 7, 1), ('st', 2, 'y', 6, 1), ('fw', 1, 'x', 5, 1),
-    ('fw', 0, 'y', 13, 2), ('fi', 1, 'x', 1, 1), ('st', 2, 'x', 1, 1), ('fi', 0, 'y', 9, 2),
-    ('gy1',), ('st', 3, 'g', 0, 1), ('fi', 1, 'x', 4, 1), ('fi', 1, 'z', 2, 1),
-    ('fi', 1, 'x', 5, 1), ('fi', 1, 'z', 3, 1), ('fi', 0, 'y', 13, 2), ('fi', 1, 'z', 8, 1),
-    ('st', 2, 'z', 2, 1), ('fw', 0, 'x', 11, 2), ('fi', 0, 'z', 15, 1), ('st', 1, 'z', 15, 1),
-    ('fi', 1, 'y', 7, 1), ('st', 1, 'y', 9, 1), ('st', 2, 'y', 7, 1), ('st', 1, 'y', 10, 1),
-    ('st', 1, 'y', 13, 1), ('st', 2, 'z', 3, 1), ('st', 1, 'y', 14, 1), ('fi', 0, 'x', 11, 2),
-    ('fw', 2, 'x', 0, 1), ('fw', 2, 'y', 6, 1), ('fw', 1, 'y', 9, 1), ('fw', 1, 'z', 15, 1),
-    ('fw', 1, 'y', 10, 1), ('st', 1, 'x', 11, 1), ('fw', 1, 'y', 13, 1), ('fw', 1, 'y', 14, 1),
-    ('fw', 2, 'x', 1, 1), ('st', 1, 'x', 12, 1), ('fw', 2, 'y', 7, 1), ('fw', 2, 'z', 2, 1),
-    ('fi', 2, 'x', 0, 1), ('st', 2, 'x', 4, 1), ('mm', 0), ('em', 0),
-    ('st', 2, 'z', 8, 1), ('fi', 1, 'z', 15, 1), ('fi', 1, 'y', 9, 1), ('st', 2, 'y', 9, 1),
-    ('fi', 1, 'y', 10, 1), ('fi', 2, 'y', 6, 1), ('fi', 1, 'y', 13, 1), ('mm', 6),
-    ('em', 6), ('st', 2, 'y', 10, 1), ('fi', 1, 'y', 14, 1), ('fi', 2, 'y', 7, 1),
-    ('mm', 7), ('em', 7), ('st', 2, 'x', 5, 1), ('fi', 2, 'x', 1, 1),
-    ('mm', 1), ('em', 1), ('fw', 1, 'x', 11, 1), ('fw', 1, 'x', 12, 1),
-    ('fi', 2, 'z', 2, 1), ('mm', 2), ('em', 2), ('fw', 2, 'z', 3, 1),
-    ('fw', 2, 'y', 9, 1), ('fw', 2, 'x', 4, 1), ('st', 2, 'z', 15, 1), ('st', 2, 'y', 13, 1),
-    ('fi', 1, 'x', 11, 1), ('fi', 1, 'x', 12, 1), ('st', 2, 'x', 11, 1), ('fi', 2, 'z', 3, 1),
-    ('fw', 2, 'z', 8, 1), ('mm', 3), ('em', 3), ('fw', 2, 'y', 10, 1),
-    ('fi', 2, 'y', 9, 1), ('mm', 9), ('em', 9), ('fw', 2, 'x', 5, 1),
-    ('fw', 3, 'g', 0, 1), ('fi', 2, 'x', 4, 1), ('mm', 4), ('em', 4),
-    ('st', 2, 'y', 14, 1), ('fw', 2, 'z', 15, 1), ('st', 2, 'x', 12, 1), ('fi', 2, 'z', 8, 1),
-    ('st', 3, 'g', 1, 1), ('mm', 8), ('em', 8), ('fw', 2, 'y', 13, 1),
-    ('fi', 2, 'y', 10, 1), ('mm', 10), ('em', 10), ('fw', 2, 'x', 11, 1),
-    ('fi', 3, 'g', 0, 1), ('fi', 2, 'x', 5, 1), ('mm', 5), ('em', 5),
-    ('fi', 2, 'z', 15, 1), ('mm', 15), ('em', 15), ('fw', 2, 'y', 14, 1),
-    ('fw', 2, 'x', 12, 1), ('fi', 2, 'y', 13, 1), ('mm', 13), ('em', 13),
-    ('fw', 3, 'g', 1, 1), ('fi', 2, 'x', 11, 1), ('mm', 11), ('em', 11),
-    ('fi', 2, 'y', 14, 1), ('mm', 14), ('em', 14), ('fi', 2, 'x', 12, 1),
-    ('mm', 12), ('em', 12), ('fi', 3, 'g', 1, 1),
+    ('rs', 0), ('rs', 1), ('rs2', 0), ('rs', 2),
+    ('norm', 0), ('norm', 1), ('norm', 2), ('rs2', 1),
+    ('rs', 3), ('norm', 3), ('upd', 0), ('st', 0, 'z', 3, 2),
+    ('st', 0, 'x', 0, 1), ('st', 0, 'y', 1, 2), ('rs2', 2), ('dd', 0),
+    ('upd', 1), ('st', 0, 'z', 8, 2), ('st', 0, 'x', 5, 2), ('st', 0, 'y', 7, 1),
+    ('fi', 0, 'z', 3, 2), ('st', 1, 'z', 3, 1), ('st', 1, 'z', 4, 1), ('fi', 0, 'x', 0, 1),
+    ('st', 1, 'x', 0, 1), ('dd', 1), ('rs2', 3), ('fi', 0, 'y', 1, 2),
+    ('st', 1, 'y', 1, 1), ('st', 1, 'y', 2, 1), ('upd', 2), ('st', 0, 'x', 10, 1),
+    ('st', 0, 'y', 11, 1), ('fi', 0, 'y', 7, 1), ('st', 1, 'y', 7, 1), ('fi', 0, 'x', 5, 2),
+    ('st', 1, 'x', 5, 1), ('st', 1, 'x', 6, 1), ('fi', 0, 'z', 8, 2), ('st', 1, 'z', 8, 1),
+    ('st', 1, 'z', 9, 1), ('fw', 1, 'z', 3, 1), ('fw', 1, 'x', 0, 1), ('dd', 2),
+    ('fw', 1, 'z', 4, 1), ('fw', 1, 'y', 1, 1), ('upd', 3), ('st', 0, 'x', 12, 2),
+    ('gy0',), ('st', 0, 'y', 14, 2), ('fi', 0, 'y', 11, 1), ('st', 1, 'y', 11, 1),
+    ('fi', 0, 'x', 10, 1), ('st', 1, 'x', 10, 1), ('fw', 1, 'y', 2, 1), ('fw', 1, 'x', 5, 1),
+    ('fw', 1, 'z', 8, 1), ('fw', 1, 'y', 7, 1), ('fw', 1, 'x', 6, 1), ('fi', 1, 'y', 1, 1),
+    ('st', 2, 'y', 1, 1), ('dd', 3), ('fi', 1, 'x', 0, 1), ('st', 2, 'x', 0, 1),
+    ('fi', 1, 'z', 3, 1), ('st', 2, 'z', 3, 1), ('fi', 1, 'z', 4, 1), ('fw', 1, 'z', 9, 1),
+    ('fi', 0, 'y', 14, 2), ('fw', 1, 'y', 11, 1), ('fi', 1, 'y', 2, 1), ('st', 2, 'y', 2, 1),
+    ('st', 1, 'y', 14, 1), ('fi', 0, 'x', 12, 2), ('fi', 1, 'y', 7, 1), ('fi', 1, 'x', 5, 1),
+    ('fw', 1, 'x', 10, 1), ('fi', 1, 'x', 6, 1), ('st', 1, 'y', 15, 1), ('st', 1, 'x', 12, 1),
+    ('gy1',), ('st', 2, 'x', 5, 1), ('st', 2, 'y', 7, 1), ('st', 1, 'x', 13, 1),
+    ('st', 2, 'z', 4, 1), ('fi', 1, 'z', 8, 1), ('fi', 1, 'y', 11, 1), ('fi', 1, 'x', 10, 1),
+    ('fw', 1, 'y', 14, 1), ('fw', 2, 'x', 0, 1), ('st', 2, 'y', 11, 1), ('fw', 1, 'x', 12, 1),
+    ('fw', 1, 'x', 13, 1), ('fw', 2, 'z', 3, 1), ('fi', 1, 'z', 9, 1), ('fw', 1, 'y', 15, 1),
+    ('fw', 2, 'x', 5, 1), ('st', 2, 'z', 8, 1), ('fi', 1, 'y', 14, 1), ('st', 2, 'x', 6, 1),
+    ('fw', 2, 'y', 1, 1), ('fi', 1, 'x', 12, 1), ('fi', 1, 'x', 13, 1), ('fi', 2, 'x', 0, 1),
+    ('mm', 0), ('em', 0), ('fw', 2, 'z', 4, 1), ('fi', 1, 'y', 15, 1),
+    ('fi', 2, 'z', 3, 1), ('mm', 3), ('em', 3), ('st', 2, 'x', 10, 1),
+    ('fw', 2, 'y', 2, 1), ('fi', 2, 'x', 5, 1), ('mm', 5), ('em', 5),
+    ('st', 2, 'z', 9, 1), ('fw', 2, 'y', 7, 1), ('fw', 2, 'x', 6, 1), ('st', 2, 'y', 14, 1),
+    ('fi', 2, 'y', 1, 1), ('fw', 2, 'z', 8, 1), ('fi', 2, 'z', 4, 1), ('mm', 1),
+    ('em', 1), ('st', 2, 'x', 12, 1), ('mm', 4), ('em', 4),
+    ('st', 3, 'g', 0, 1), ('fi', 2, 'y', 2, 1), ('mm', 2), ('em', 2),
+    ('fw', 2, 'y', 11, 1), ('fi', 2, 'y', 7, 1), ('mm', 7), ('em', 7),
+    ('fw', 2, 'x', 10, 1), ('st', 2, 'y', 15, 1), ('fi', 2, 'x', 6, 1), ('fw', 2, 'z', 9, 1),
+    ('mm', 6), ('em', 6), ('st', 2, 'x', 13, 1), ('fi', 2, 'z', 8, 1),
+    ('mm', 8), ('em', 8), ('st', 3, 'g', 1, 1), ('fw', 2, 'y', 14, 1),
+    ('fi', 2, 'y', 11, 1), ('mm', 11), ('em', 11), ('fw', 2, 'x', 12, 1),
+    ('fi', 2, 'x', 10, 1), ('fw', 3, 'g', 0, 1), ('mm', 10), ('em', 10),
+    ('fi', 2, 'z', 9, 1), ('mm', 9), ('em', 9), ('fw', 2, 'y', 15, 1),
+    ('fw', 2, 'x', 13, 1), ('fw', 3, 'g', 1, 1), ('fi', 2, 'y', 14, 1), ('mm', 14),
+    ('em', 14), ('fi', 2, 'x', 12, 1), ('mm', 12), ('em', 12),
+    ('fi', 3, 'g', 0, 1), ('fi', 2, 'y', 15, 1), ('mm', 15), ('em', 15),
+    ('fi', 2, 'x', 13, 1), ('mm', 13), ('em', 13), ('fi', 3, 'g', 1, 1),
 )
 
 
@@ -77,9 +76,9 @@
 
 
 def kernel(
-    tokens, gain, params, moment, deltas, hidden, grads,
-    wts, tok, normed, own0, own1, ry0, rz0, rz1, ry1, pz0, pz1, pbuf, mbuf, gsum, stage, hbuf,
-    loc, a_s, a_r, b_s, b_r, tk_s, tk_r, dd_s, dd_r, ring_s, ring_r, gy_s, gy_r, h_l, h_s, h_r,
+    tokens, gain_in, params, moment, deltas, hidden, grads,
+    gain, wts, tok, normed, own0, own1, ry0, rz0, rz1, ry1, pz0, pz1, pbuf, mbuf, gsum, stage, hbuf,
+    loc, a_s, a_r, b_s, b_r, tk_s, tk_r, dd_s, dd_r, line_s, line_r, ring_s, ring_r, gy_s, gy_r, h_l, h_s, h_r,
 ):
     bf16, f32 = jnp.bfloat16, jnp.float32
     rep = lax.axis_index("rep")
@@ -88,8 +87,8 @@
     yh, x, core = fsdp // 8, (fsdp // 2) % 4, fsdp % 2
     here = {"x": x, "y": yh * 2 + yl, "z": z}
 
-    def device(at):
-        return (at["z"] * 2 + at["y"] % 2, (at["y"] // 2) * 8 + at["x"] * 2 + core)
+    def device(at, c=core):
+        return (at["z"] * 2 + at["y"] % 2, (at["y"] // 2) * 8 + at["x"] * 2 + c)
 
     def shifted(axis, step):
         return {**here, axis: (here[axis] + step + 4) % 4}
@@ -104,7 +103,7 @@
         return (zpos(dz) * 2 + yl, fsdp)
 
     barrier = pltpu.get_barrier_semaphore()
-    greet = [device(shifted(a, d)) for a in "xyz" for d in (1, -1)] + [zdev(2), partner]
+    greet = [device(shifted(a, d), c) for a in "xyz" for d in (1, 2, 3) for c in (core, 1 - core)] + [partner]
     for who in greet:
         pl.semaphore_signal(barrier, inc=1, device_id=who, device_id_type=MESH)
     loads = [
@@ -113,6 +112,7 @@
         pltpu.make_async_copy(deltas.at[1, z], own1, loc.at[2]),
         pltpu.make_async_copy(params.at[:, rep], pbuf, loc.at[3]),
         pltpu.make_async_copy(moment.at[:, rep], mbuf, loc.at[4]),
+        pltpu.make_async_copy(gain_in, gain, loc.at[6]),
     ]
     for c in loads:
         c.start()
@@ -171,7 +171,7 @@
 
     def do_rs2(s):
         if s == 0:
-            for c in loads[1:]:
+            for c in loads[1:-1]:
                 c.wait()
         for _, dst, i, who in first_hop(s):
             landed(dst, a_s.at[i], a_r.at[i], who)
@@ -230,11 +230,25 @@
         fh, fl = (ALL, ALL) if at["y"] is None else (at["y"] // 2, at["y"] % 2)
         return wts.at[us, fh, fx, half, fz, fl]
 
+    def lines(part, first, count):
+        axis = ORDERS[part][0]
+        us = pl.ds(first, count)
+        for i, step in enumerate((2, 1, 3)):
+            for k in range(2):
+                row = core if k == 0 else 1 - core
+                at = shifted(axis, -step)
+                lands = wts.at[us, at["y"] // 2, at["x"], row, at["z"], at["y"] % 2]
+                mine = wts.at[us, yh, x, core, z, yl]
+                yield (mine if k == 0 else stage.at[us]), mine, lands, (
+                    line_s.at[first, 2 * i + k], line_r.at[first, 2 * i + k], device(shifted(axis, step), row))
+
     def ring(phase, part, first, count):
         order = ORDERS[part]
         axis = order[phase]
-        row = phase * UNITS + first
-        to = [device(shifted(axis, d)) for d in (1, -1)]
+        row = (phase - 1) * UNITS + first
+        toward = 1 - 2 * yl if axis == "y" else 1
+        steps = (toward, -toward)
+        to = [device(shifted(axis, d)) for d in steps]
 
         def block(step, half=ALL):
             if part == "g":
@@ -247,24 +261,41 @@
         def sems(i):
             return (ring_s.at[row, i], ring_r.at[row, i], to[i % 2])
 
-        return block, sems
-
-    def do_st(*what):
-        block, sems = ring(*what)
+        came = steps if axis == "y" else (-steps[0], -steps[1])
+        onward = (1, 0) if axis == "y" else (0, 1)
+        if axis == "y" and first in SKEWED:
+            carried = (None, ALL)
+        else:
+            carried = (0, 1)
+        return block, sems, came, onward, carried
+
+    def do_st(phase, part, first, count):
+        if phase == 0:
+            for src, dst, _, where in lines(part, first, count):
+                send(src, dst, *where)
+            return
+        block, sems, _, _, _ = ring(phase, part, first, count)
         for d in range(2):
             send(block(0), block(0), *sems(d))
 
     def do_fw(*what):
-        block, sems = ring(*what)
+        block, sems, came, onward, carried = ring(*what)
         for d in range(2):
-            back = -1 if d == 0 else 1
-            landed(block(back), *sems(d))
-            send(block(back, d), block(back, d), *sems(2 + d))
-
-    def do_fi(*what):
-        block, sems = ring(*what)
+            landed(block(came[d]), *sems(d))
+            half = carried[onward[d]]
+            if half is not None:
+                part = block(came[d], half)
+                send(part, part, *sems(2 + onward[d]))
+
+    def do_fi(phase, part, first, count):
+        if phase == 0:
+            for _, _, lands, where in lines(part, first, count):
+                landed(lands, *where)
+            return
+        block, sems, _, _, carried = ring(phase, part, first, count)
         for d in range(2):
-            landed(block(2, d), *sems(2 + d))
+            if carried[d] is not None:
+                landed(block(2, carried[d]), *sems(2 + d))
 
     def do_gy0():
         own = gsum.at[:, z, yl]
@@ -279,6 +310,7 @@
         count = 1024 // NORMS
         if not waited:
             loads[0].wait()
+            loads[-1].wait()
             waited.append(0)
         if len(waited) == 1 and (part + 1) * count > 512:
             landed(tok.at[1], tk_s, tk_r, partner)
@@ -338,6 +370,10 @@
         landed(hidden_cols(1 - core, u), h_s.at[u], h_r.at[u], partner)
     for c in sent:
         c.wait_send()
+
+
+def held(a):
+    return pltpu.with_memory_space_constraint(a, pltpu.HBM)
 
 
 def body(tokens, norm_gain, outer_params, momentum, deltas):
@@ -352,9 +388,10 @@
             jax.ShapeDtypeStruct((512, 4096), bf16),
             jax.ShapeDtypeStruct((2, 4, 2, 16, 4096), bf16),
         ),
-        in_specs=[hbm, pl.BlockSpec(memory_space=pltpu.VMEM), hbm, hbm, hbm],
+        in_specs=[hbm] * 5,
         out_specs=(hbm, hbm),
         scratch_shapes=[
+            vmem((1, 2048), f32),
             vmem((UNITS, 2, 4, 2, 4, 2, 16, 2 * LANES), bf16),
             vmem((2, 512, 2048), bf16),
             vmem((1024, 2048), bf16),
@@ -371,25 +408,26 @@
             vmem((2, 4, 2, 16, 4096), bf16),
             vmem((UNITS, 16, 2 * LANES), bf16),
             vmem((UNITS, 2, 512, LANES), bf16),
-            dma((6,)),
+            dma((7,)),
             dma((spans, 2, 4)), dma((spans, 2, 4)),
             dma((spans, 2, 4)), dma((spans, 2, 4)),
             dma, dma,
             dma((spans,)), dma((spans,)),
-            dma((3 * UNITS + PIECES, 4)), dma((3 * UNITS + PIECES, 4)),
+            dma((UNITS, 6)), dma((UNITS, 6)),
+            dma((2 * UNITS + PIECES, 4)), dma((2 * UNITS + PIECES, 4)),
             dma, dma,
             dma((UNITS,)), dma((UNITS,)), dma((UNITS,)),
         ],
         compiler_params=pltpu.CompilerParams(
-            collective_id=0, has_side_effects=True, vmem_limit_bytes=62 * 1024 * 1024
+            collective_id=0, has_side_effects=True, vmem_limit_bytes=44 * 1024 * 1024
         ),
         name="outer_round",
     )(
-        tokens,
-        norm_gain.reshape(1, 2048),
-        outer_params.reshape(2, 8, 16, 4096),
-        momentum.reshape(2, 8, 16, 4096),
-        deltas.reshape(2, 4, 2, 16, 4096),
+        held(tokens),
+        held(norm_gain.reshape(1, 2048)),
+        held(outer_params.reshape(2, 8, 16, 4096)),
+        held(momentum.reshape(2, 8, 16, 4096)),
+        held(deltas.reshape(2, 4, 2, 16, 4096)),
     )
     outer_grad = grads.reshape(2, 128, 4096).astype(f32)
     new_params, new_momentum = advance(outer_params, momentum, outer_grad)

time: 119 us -> 112 us (0.941)
  other arithmetic: 9.45 us -> 5.4 us
  Pallas kernels: 107 us -> 104 us
    sub x1, other arithmetic: 9.45 us -> 5.4 us  [advance(): params_next = params - RATE * (outer_grad + MU * moment_next)]
    pallas_call x1, Pallas kernels: 107 us -> 104 us  [body(): pl.pallas_call(kernel, out_shape=(jax.ShapeDtypeStruct((512, 4096), bf16)...]
where the time goes in v3:
time: 112 us
  Pallas kernels  104 us (93%)
  other arithmetic  5.4 us (5%)
  local copies, waits for them, and re-layouts  2.02 us (2%)
    pallas_call x1, Pallas kernels, body(): pl.pallas_call(kernel, out_shape=(jax.ShapeDtypeStruct((512, 4096), bf16)...  104 us
    sub x1, other arithmetic, advance(): params_next = params - RATE * (outer_grad + MU * moment_next)  5.4 us

profile of v3, /device:TPU:1, one launch (start us, length us, event | category | flops | bytes accessed | tf_op | source)
XLA Modules:
  0.0 111.9 jit_solution(9045140493498752336)
XLA Ops:
  0.6 0.0 copy-start
  0.6 0.0 copy-start.1
  0.7 103.8 %outer_round.1 = (bf16[512,4096]{1,0:T(8,128)(2,1)S(1)}, bf16[2,4,2,16,4096]{4,3,2,1,0:T(8,128)(2,1)S(1)}) custom-call(bf16[512,2048]{1,0:T(8,128)(2,1)} %tokens.1, f32[1,2048]{1,0:T(1,128)} %bitcast.12, f32[2,8,16,4096]{3,2,1,0:T(8,128)} %bitcast.9, f32[2,8,16,4096]{3,2,1,0:T(8,128)} %bitcast.10, bf16[2,4,2,16,4096]{4,3,2,1,0:T(8,128)(2,1)} %bitcast.11), custom_call_target="tpu_custom_call" | custom-call | tf_op jit(solution)/shard_map/outer_round/pallas_call | solution.py:385
  104.5 0.0 copy-done
  104.5 0.0 copy-done.1
  104.5 5.4 %fusion.1 = (f32[2,128,4096]{2,1,0:T(8,128)}, f32[2,128,4096]{2,1,0:T(8,128)}) fusion(f32[2,128,4096]{2,1,0:T(8,128)S(1)} %copy-done, bf16[2,4,2,16,4096]{4,3,2,1,0:T(8,128)(2,1)S(1)} %get-tuple-element.5, f32[2,128,4096]{2,1,0:T(8,128)S(1)} %copy-done.1), kind=kLoop, calls=%fused_computation.3 | loop fusion | flops 7340032 | bytes 18874368 | tf_op jit(solution)/shard_map/sub | solution.py:74
  109.9 2.0 %copy.9 = bf16[512,4096]{1,0:T(8,128)(2,1)} copy(bf16[512,4096]{1,0:T(8,128)(2,1)S(1)} %get-tuple-element.14) | data formatting | bytes 8388608
Async XLA Ops:
  0.6 103.9 %copy-start = (f32[2,128,4096]{2,1,0:T(8,128)S(1)}, f32[2,128,4096]{2,1,0:T(8,128)}, u32[]{:S(2)}) copy-start(f32[2,128,4096]{2,1,0:T(8,128)} %param.7) | copy-start | bytes 12582916
  0.6 103.9 %copy-start.1 = (f32[2,128,4096]{2,1,0:T(8,128)S(1)}, f32[2,128,4096]{2,1,0:T(8,128)}, u32[]{:S(2)}) copy-start(f32[2,128,4096]{2,1,0:T(8,128)} %param.8) | copy-start | bytes 12582916

commit v4 on v3

--- a/solution.py
+++ b/solution.py
@@ -370,6 +370,23 @@
         landed(hidden_cols(1 - core, u), h_s.at[u], h_r.at[u], partner)
     for c in sent:
         c.wait_send()
+
+
+def finish(params, moment, grads, rows, params_out, moment_out, rows_out, pbuf, mbuf, sems):
+    copies = [pltpu.make_async_copy(rows, rows_out, sems.at[0, 0])]
+    copies[0].start()
+    for mat in range(2):
+        for i in range(8):
+            at = pl.ds(i * 16, 16)
+            g = grads[mat, at, :].astype(jnp.float32)
+            new, nxt = advance(params[mat, at, :], moment[mat, at, :], g)
+            pbuf[mat, at, :] = new
+            mbuf[mat, at, :] = nxt
+            for k, (src, dst) in enumerate(((pbuf, params_out), (mbuf, moment_out))):
+                copies.append(pltpu.make_async_copy(src.at[mat, at], dst.at[mat, at], sems.at[1 + k, mat * 8 + i]))
+                copies[-1].start()
+    for c in copies:
+        c.wait()
 
 
 def held(a):
@@ -429,9 +446,17 @@
         held(momentum.reshape(2, 8, 16, 4096)),
         held(deltas.reshape(2, 4, 2, 16, 4096)),
     )
-    outer_grad = grads.reshape(2, 128, 4096).astype(f32)
-    new_params, new_momentum = advance(outer_params, momentum, outer_grad)
-    return (new_params, new_momentum, hidden)
+    here = pl.BlockSpec(memory_space=pltpu.VMEM)
+    state = jax.ShapeDtypeStruct((2, 128, 4096), f32)
+    return pl.pallas_call(
+        finish,
+        out_shape=(state, state, jax.ShapeDtypeStruct((512, 4096), bf16)),
+        in_specs=[here] * 4,
+        out_specs=(hbm, hbm, hbm),
+        scratch_shapes=[vmem((2, 128, 4096), f32), vmem((2, 128, 4096), f32), dma((3, 16))],
+        compiler_params=pltpu.CompilerParams(vmem_limit_bytes=28 * 1024 * 1024),
+        name="finish",
+    )(outer_params, momentum, grads.reshape(2, 128, 4096), hidden)
 
 
 def solution(mesh):

time: 112 us -> 110 us (0.982)
  other arithmetic: 5.4 us -> 0 us
  Pallas kernels: 104 us -> 109 us
  local copies, waits for them, and re-layouts: 2.02 us -> 0.01 us
    sub x1 -> x0, other arithmetic: 5.4 us -> none  [advance(): params_next = params - RATE * (outer_grad + MU * moment_next)]
    pallas_call x0 -> x1, Pallas kernels: none -> 4.94 us  [body(): pl.pallas_call(finish, out_shape=(state, state, jax.ShapeDtypeStruct((512...]
    unnamed x5 -> x4, local copies, waits for them, and re-layouts: 2.02 us -> 0.01 us
where the time goes in v4:
time: 110 us
  Pallas kernels  109 us (99%)
    pallas_call x1, Pallas kernels, body(): pl.pallas_call(kernel, out_shape=(jax.ShapeDtypeStruct((512, 4096), bf16)...  104 us
    pallas_call x1, Pallas kernels, body(): pl.pallas_call(finish, out_shape=(state, state, jax.ShapeDtypeStruct((512...  4.94 us

profile of v4, /device:TPU:1, one launch (start us, length us, event | category | flops | bytes accessed | tf_op | source)
XLA Modules:
  0.0 109.6 jit_solution(2546546634561203051)
XLA Ops:
  0.6 0.0 copy-start
  0.6 0.0 copy-start.1
  0.7 103.8 %outer_round.1 = (bf16[512,4096]{1,0:T(8,128)(2,1)S(1)}, bf16[2,4,2,16,4096]{4,3,2,1,0:T(8,128)(2,1)S(1)}) custom-call(bf16[512,2048]{1,0:T(8,128)(2,1)} %tokens.1, f32[1,2048]{1,0:T(1,128)} %bitcast.9, f32[2,8,16,4096]{3,2,1,0:T(8,128)} %bitcast.5, f32[2,8,16,4096]{3,2,1,0:T(8,128)} %bitcast.6, bf16[2,4,2,16,4096]{4,3,2,1,0:T(8,128)(2,1)} %bitcast.8), custom_call_target="tpu_custom_call" | custom-call | tf_op jit(solution)/shard_map/outer_round/pallas_call | solution.py:402
  104.5 0.0 copy-done
  104.5 0.0 copy-done.1
  104.5 4.9 %finish.1 = (f32[2,128,4096]{2,1,0:T(8,128)}, f32[2,128,4096]{2,1,0:T(8,128)}, bf16[512,4096]{1,0:T(8,128)(2,1)}) custom-call(f32[2,128,4096]{2,1,0:T(8,128)S(1)} %copy-done, f32[2,128,4096]{2,1,0:T(8,128)S(1)} %copy-done.1, bf16[2,128,4096]{2,1,0:T(8,128)(2,1)S(1)} %bitcast.7, bf16[512,4096]{1,0:T(8,128)(2,1)S(1)} %get-tuple-element.6.rows), custom_call_target="tpu_custom_call" | custom-call | tf_op jit(solution)/shard_map/finish/pallas_call | solution.py:451
Async XLA Ops:
  0.6 103.9 %copy-start = (f32[2,128,4096]{2,1,0:T(8,128)S(1)}, f32[2,128,4096]{2,1,0:T(8,128)}, u32[]{:S(2)}) copy-start(f32[2,128,4096]{2,1,0:T(8,128)} %params.1) | copy-start | bytes 12582916
  0.6 103.9 %copy-start.1 = (f32[2,128,4096]{2,1,0:T(8,128)S(1)}, f32[2,128,4096]{2,1,0:T(8,128)}, u32[]{:S(2)}) copy-start(f32[2,128,4096]{2,1,0:T(8,128)} %moment.1) | copy-start | bytes 12582916

commit v5 on v4

--- a/solution.py
+++ b/solution.py
@@ -17,54 +17,56 @@
 HALF = 2048
 
 ORDERS = {'x': ('y', 'z', 'x'), 'y': ('z', 'x', 'y'), 'z': ('x', 'y', 'z'), 'g': ('z', 'z', 'z', 'z')}
-SPANS = ((0, 5), (5, 5), (10, 2), (12, 4))
+SPANS = ((0, 3), (3, 4), (7, 3), (10, 3), (13, 3))
 PIECES = 2
-NORMS = 4
-SKEWED = (1, 5, 6, 13)
+NORMS = 2
+SKEWED = (2, 7, 8, 10, 11, 13)
 PLAN = (
     ('rs', 0), ('rs', 1), ('rs2', 0), ('rs', 2),
-    ('norm', 0), ('norm', 1), ('norm', 2), ('rs2', 1),
-    ('rs', 3), ('norm', 3), ('upd', 0), ('st', 0, 'z', 3, 2),
-    ('st', 0, 'x', 0, 1), ('st', 0, 'y', 1, 2), ('rs2', 2), ('dd', 0),
-    ('upd', 1), ('st', 0, 'z', 8, 2), ('st', 0, 'x', 5, 2), ('st', 0, 'y', 7, 1),
-    ('fi', 0, 'z', 3, 2), ('st', 1, 'z', 3, 1), ('st', 1, 'z', 4, 1), ('fi', 0, 'x', 0, 1),
-    ('st', 1, 'x', 0, 1), ('dd', 1), ('rs2', 3), ('fi', 0, 'y', 1, 2),
-    ('st', 1, 'y', 1, 1), ('st', 1, 'y', 2, 1), ('upd', 2), ('st', 0, 'x', 10, 1),
-    ('st', 0, 'y', 11, 1), ('fi', 0, 'y', 7, 1), ('st', 1, 'y', 7, 1), ('fi', 0, 'x', 5, 2),
-    ('st', 1, 'x', 5, 1), ('st', 1, 'x', 6, 1), ('fi', 0, 'z', 8, 2), ('st', 1, 'z', 8, 1),
-    ('st', 1, 'z', 9, 1), ('fw', 1, 'z', 3, 1), ('fw', 1, 'x', 0, 1), ('dd', 2),
-    ('fw', 1, 'z', 4, 1), ('fw', 1, 'y', 1, 1), ('upd', 3), ('st', 0, 'x', 12, 2),
-    ('gy0',), ('st', 0, 'y', 14, 2), ('fi', 0, 'y', 11, 1), ('st', 1, 'y', 11, 1),
-    ('fi', 0, 'x', 10, 1), ('st', 1, 'x', 10, 1), ('fw', 1, 'y', 2, 1), ('fw', 1, 'x', 5, 1),
-    ('fw', 1, 'z', 8, 1), ('fw', 1, 'y', 7, 1), ('fw', 1, 'x', 6, 1), ('fi', 1, 'y', 1, 1),
-    ('st', 2, 'y', 1, 1), ('dd', 3), ('fi', 1, 'x', 0, 1), ('st', 2, 'x', 0, 1),
-    ('fi', 1, 'z', 3, 1), ('st', 2, 'z', 3, 1), ('fi', 1, 'z', 4, 1), ('fw', 1, 'z', 9, 1),
-    ('fi', 0, 'y', 14, 2), ('fw', 1, 'y', 11, 1), ('fi', 1, 'y', 2, 1), ('st', 2, 'y', 2, 1),
-    ('st', 1, 'y', 14, 1), ('fi', 0, 'x', 12, 2), ('fi', 1, 'y', 7, 1), ('fi', 1, 'x', 5, 1),
-    ('fw', 1, 'x', 10, 1), ('fi', 1, 'x', 6, 1), ('st', 1, 'y', 15, 1), ('st', 1, 'x', 12, 1),
-    ('gy1',), ('st', 2, 'x', 5, 1), ('st', 2, 'y', 7, 1), ('st', 1, 'x', 13, 1),
-    ('st', 2, 'z', 4, 1), ('fi', 1, 'z', 8, 1), ('fi', 1, 'y', 11, 1), ('fi', 1, 'x', 10, 1),
-    ('fw', 1, 'y', 14, 1), ('fw', 2, 'x', 0, 1), ('st', 2, 'y', 11, 1), ('fw', 1, 'x', 12, 1),
-    ('fw', 1, 'x', 13, 1), ('fw', 2, 'z', 3, 1), ('fi', 1, 'z', 9, 1), ('fw', 1, 'y', 15, 1),
-    ('fw', 2, 'x', 5, 1), ('st', 2, 'z', 8, 1), ('fi', 1, 'y', 14, 1), ('st', 2, 'x', 6, 1),
-    ('fw', 2, 'y', 1, 1), ('fi', 1, 'x', 12, 1), ('fi', 1, 'x', 13, 1), ('fi', 2, 'x', 0, 1),
-    ('mm', 0), ('em', 0), ('fw', 2, 'z', 4, 1), ('fi', 1, 'y', 15, 1),
-    ('fi', 2, 'z', 3, 1), ('mm', 3), ('em', 3), ('st', 2, 'x', 10, 1),
-    ('fw', 2, 'y', 2, 1), ('fi', 2, 'x', 5, 1), ('mm', 5), ('em', 5),
-    ('st', 2, 'z', 9, 1), ('fw', 2, 'y', 7, 1), ('fw', 2, 'x', 6, 1), ('st', 2, 'y', 14, 1),
-    ('fi', 2, 'y', 1, 1), ('fw', 2, 'z', 8, 1), ('fi', 2, 'z', 4, 1), ('mm', 1),
-    ('em', 1), ('st', 2, 'x', 12, 1), ('mm', 4), ('em', 4),
-    ('st', 3, 'g', 0, 1), ('fi', 2, 'y', 2, 1), ('mm', 2), ('em', 2),
-    ('fw', 2, 'y', 11, 1), ('fi', 2, 'y', 7, 1), ('mm', 7), ('em', 7),
-    ('fw', 2, 'x', 10, 1), ('st', 2, 'y', 15, 1), ('fi', 2, 'x', 6, 1), ('fw', 2, 'z', 9, 1),
-    ('mm', 6), ('em', 6), ('st', 2, 'x', 13, 1), ('fi', 2, 'z', 8, 1),
-    ('mm', 8), ('em', 8), ('st', 3, 'g', 1, 1), ('fw', 2, 'y', 14, 1),
-    ('fi', 2, 'y', 11, 1), ('mm', 11), ('em', 11), ('fw', 2, 'x', 12, 1),
-    ('fi', 2, 'x', 10, 1), ('fw', 3, 'g', 0, 1), ('mm', 10), ('em', 10),
-    ('fi', 2, 'z', 9, 1), ('mm', 9), ('em', 9), ('fw', 2, 'y', 15, 1),
-    ('fw', 2, 'x', 13, 1), ('fw', 3, 'g', 1, 1), ('fi', 2, 'y', 14, 1), ('mm', 14),
-    ('em', 14), ('fi', 2, 'x', 12, 1), ('mm', 12), ('em', 12),
-    ('fi', 3, 'g', 0, 1), ('fi', 2, 'y', 15, 1), ('mm', 15), ('em', 15),
+    ('norm', 0), ('rs2', 1), ('rs', 3), ('norm', 1),
+    ('upd', 0), ('st', 0, 'z', 2, 1), ('st', 0, 'x', 0, 1), ('st', 0, 'y', 1, 1),
+    ('rs2', 2), ('rs', 4), ('dd', 0), ('upd', 1),
+    ('st', 0, 'z', 5, 2), ('st', 0, 'x', 3, 1), ('st', 0, 'y', 4, 1), ('fi', 0, 'z', 2, 1),
+    ('st', 1, 'z', 2, 1), ('fi', 0, 'x', 0, 1), ('st', 1, 'x', 0, 1), ('rs2', 3),
+    ('fi', 0, 'y', 1, 1), ('st', 1, 'y', 1, 1), ('dd', 1), ('upd', 2),
+    ('st', 0, 'z', 9, 1), ('st', 0, 'x', 7, 1), ('st', 0, 'y', 8, 1), ('fi', 0, 'z', 5, 2),
+    ('st', 1, 'z', 5, 1), ('st', 1, 'z', 6, 1), ('fi', 0, 'x', 3, 1), ('st', 1, 'x', 3, 1),
+    ('rs2', 4), ('fi', 0, 'y', 4, 1), ('st', 1, 'y', 4, 1), ('dd', 2),
+    ('fw', 1, 'y', 1, 1), ('fw', 1, 'z', 2, 1), ('fw', 1, 'x', 0, 1), ('fi', 0, 'x', 7, 1),
+    ('st', 1, 'x', 7, 1), ('fi', 0, 'z', 9, 1), ('st', 1, 'z', 9, 1), ('upd', 3),
+    ('st', 0, 'x', 10, 2), ('st', 0, 'y', 12, 1), ('fi', 0, 'y', 8, 1), ('st', 1, 'y', 8, 1),
+    ('fw', 1, 'z', 5, 1), ('fw', 1, 'x', 3, 1), ('fw', 1, 'y', 4, 1), ('fw', 1, 'z', 6, 1),
+    ('fi', 1, 'y', 1, 1), ('st', 2, 'y', 1, 1), ('dd', 3), ('fi', 1, 'x', 0, 1),
+    ('st', 2, 'x', 0, 1), ('fi', 1, 'z', 2, 1), ('st', 2, 'z', 2, 1), ('upd', 4),
+    ('fw', 1, 'y', 8, 1), ('fi', 1, 'y', 4, 1), ('st', 0, 'y', 14, 2), ('fi', 1, 'x', 3, 1),
+    ('st', 2, 'x', 3, 1), ('st', 0, 'x', 13, 1), ('fi', 0, 'y', 12, 1), ('dd', 4),
+    ('fi', 1, 'z', 5, 1), ('fw', 1, 'z', 9, 1), ('fw', 1, 'x', 7, 1), ('fi', 0, 'x', 10, 2),
+    ('st', 2, 'y', 4, 1), ('st', 1, 'x', 10, 1), ('fi', 1, 'z', 6, 1), ('st', 1, 'y', 12, 1),
+    ('st', 1, 'x', 11, 1), ('st', 2, 'z', 5, 1), ('fi', 1, 'y', 8, 1), ('fw', 2, 'x', 0, 1),
+    ('fw', 2, 'y', 1, 1), ('fi', 1, 'x', 7, 1), ('fi', 0, 'y', 14, 2), ('fi', 1, 'z', 9, 1),
+    ('fi', 0, 'x', 13, 1), ('st', 1, 'y', 14, 1), ('st', 1, 'y', 15, 1), ('st', 2, 'y', 8, 1),
+    ('fw', 1, 'x', 10, 1), ('fw', 1, 'x', 11, 1), ('st', 1, 'x', 13, 1), ('fw', 1, 'y', 12, 1),
+    ('fw', 2, 'x', 3, 1), ('fw', 2, 'z', 2, 1), ('fi', 2, 'x', 0, 1), ('st', 2, 'x', 7, 1),
+    ('fw', 2, 'y', 4, 1), ('st', 2, 'z', 6, 1), ('mm', 0), ('em', 0),
+    ('gy0',), ('fi', 1, 'x', 10, 1), ('fi', 1, 'x', 11, 1), ('fi', 2, 'y', 1, 1),
+    ('fi', 1, 'y', 12, 1), ('st', 2, 'y', 12, 1), ('mm', 1), ('em', 1),
+    ('fw', 1, 'x', 13, 1), ('fi', 2, 'z', 2, 1), ('fw', 1, 'y', 14, 1), ('fw', 1, 'y', 15, 1),
+    ('fw', 2, 'z', 5, 1), ('fi', 2, 'x', 3, 1), ('st', 2, 'x', 10, 1), ('mm', 2),
+    ('em', 2), ('mm', 3), ('em', 3), ('fw', 2, 'y', 8, 1),
+    ('st', 2, 'z', 9, 1), ('fi', 2, 'y', 4, 1), ('mm', 4), ('em', 4),
+    ('fi', 1, 'x', 13, 1), ('fw', 2, 'x', 7, 1), ('fi', 1, 'y', 14, 1), ('fi', 1, 'y', 15, 1),
+    ('st', 2, 'y', 14, 1), ('gy1',), ('fw', 2, 'z', 6, 1), ('fi', 2, 'z', 5, 1),
+    ('st', 2, 'x', 11, 1), ('mm', 5), ('em', 5), ('st', 2, 'y', 15, 1),
+    ('st', 3, 'g', 0, 1), ('fi', 2, 'y', 8, 1), ('fw', 2, 'x', 10, 1), ('mm', 8),
+    ('em', 8), ('fi', 2, 'x', 7, 1), ('fw', 2, 'z', 9, 1), ('mm', 7),
+    ('em', 7), ('st', 2, 'x', 13, 1), ('fi', 2, 'z', 6, 1), ('mm', 6),
+    ('em', 6), ('fw', 2, 'y', 12, 1), ('st', 3, 'g', 1, 1), ('fw', 2, 'y', 14, 1),
+    ('fw', 2, 'x', 11, 1), ('fi', 2, 'x', 10, 1), ('mm', 10), ('em', 10),
+    ('fw', 3, 'g', 0, 1), ('fw', 2, 'y', 15, 1), ('fi', 2, 'z', 9, 1), ('mm', 9),
+    ('em', 9), ('fi', 2, 'y', 12, 1), ('mm', 12), ('em', 12),
+    ('fw', 2, 'x', 13, 1), ('fi', 2, 'y', 14, 1), ('fw', 3, 'g', 1, 1), ('mm', 14),
+    ('em', 14), ('fi', 2, 'x', 11, 1), ('mm', 11), ('em', 11),
+    ('fi', 2, 'y', 15, 1), ('fi', 3, 'g', 0, 1), ('mm', 15), ('em', 15),
     ('fi', 2, 'x', 13, 1), ('mm', 13), ('em', 13), ('fi', 3, 'g', 1, 1),
 )
 
@@ -77,7 +79,7 @@
 
 def kernel(
     tokens, gain_in, params, moment, deltas, hidden, grads,
-    gain, wts, tok, normed, own0, own1, ry0, rz0, rz1, ry1, pz0, pz1, pbuf, mbuf, gsum, stage, hbuf,
+    gain, wts, tok, normed, held, ry0, rz0, rz1, ry1, pz0, pz1, pbuf, mbuf, gsum, stage, hbuf,
     loc, a_s, a_r, b_s, b_r, tk_s, tk_r, dd_s, dd_r, line_s, line_r, ring_s, ring_r, gy_s, gy_r, h_l, h_s, h_r,
 ):
     bf16, f32 = jnp.bfloat16, jnp.float32
@@ -108,15 +110,16 @@
         pl.semaphore_signal(barrier, inc=1, device_id=who, device_id_type=MESH)
     loads = [
         pltpu.make_async_copy(tokens, tok.at[0], loc.at[0]),
-        pltpu.make_async_copy(deltas.at[0, :, yl], own0, loc.at[1]),
-        pltpu.make_async_copy(deltas.at[1, z], own1, loc.at[2]),
         pltpu.make_async_copy(params.at[:, rep], pbuf, loc.at[3]),
         pltpu.make_async_copy(moment.at[:, rep], mbuf, loc.at[4]),
         pltpu.make_async_copy(gain_in, gain, loc.at[6]),
     ]
+    staged = pltpu.make_async_copy(deltas, held, loc.at[1])
+    staged.start()
+    pl.semaphore_wait(barrier, len(greet))
     for c in loads:
         c.start()
-    pl.semaphore_wait(barrier, len(greet))
+    staged.wait()
 
     sent = []
 
@@ -141,8 +144,8 @@
         for h in range(2):
             cols = lanes_at(h, *SPANS[s])
             for dz in (2, 1, 3):
-                out.append((deltas.at[1, zpos(dz), :, :, cols], rz1.at[dz - 1, :, :, cols], (s, h, dz), zdev(dz)))
-            out.append((deltas.at[0, :, 1 - yl, :, cols], ry0.at[:, :, cols], (s, h, 0), ydev))
+                out.append((held.at[1, zpos(dz), :, :, cols], rz1.at[dz - 1, :, :, cols], (s, h, dz), zdev(dz)))
+            out.append((held.at[0, :, 1 - yl, :, cols], ry0.at[:, :, cols], (s, h, 0), ydev))
         return out
 
     def second_hop(s):
@@ -180,9 +183,9 @@
             for h in range(2):
                 cols = lanes_at(h, j, 1)
                 for dz in (1, 2, 3):
-                    v = own0[zpos(dz), :, cols].astype(f32) + ry0[zpos(dz), :, cols].astype(f32)
+                    v = held[0, zpos(dz), yl, :, cols].astype(f32) + ry0[zpos(dz), :, cols].astype(f32)
                     pz0[dz - 1, :, cols] = v.astype(bf16)
-                v = own1[1 - yl, :, cols].astype(f32)
+                v = held[1, z, 1 - yl, :, cols].astype(f32)
                 for k in range(3):
                     v = v + rz1[k, 1 - yl, :, cols].astype(f32)
                 pz1[:, cols] = v.astype(bf16)
@@ -200,11 +203,11 @@
                 cols = lanes_at((1 - core) if other else core, j, 1)
                 for mat in range(2):
                     if mat == 0:
-                        v = own0[z, :, cols].astype(f32) + ry0[z, :, cols].astype(f32)
+                        v = held[0, z, yl, :, cols].astype(f32) + ry0[z, :, cols].astype(f32)
                         for k in range(3):
                             v = v + rz0[k, :, cols].astype(f32)
                     else:
-                        v = own1[yl, :, cols].astype(f32)
+                        v = held[1, z, yl, :, cols].astype(f32)
                         for k in range(3):
                             v = v + rz1[k, yl, :, cols].astype(f32)
                         v = v + ry1[:, cols].astype(f32)
@@ -329,6 +332,8 @@
 
     factor = 1.0 / math.sqrt(2048)
 
+    last = [op[1] for op in PLAN if op[0] == "mm"][-1]
+
     def do_mm(u):
         def step(m, carry):
             rows = pl.ds(pl.multiple_of(m * 512, 512), 512)
@@ -339,9 +344,17 @@
             hbuf[u, m] = ((gate / (1.0 + jnp.exp(-gate))) * up).astype(bf16)
             return carry
 
-        lax.fori_loop(0, 2, step, 0)
+        if u == last:
+            step(1, 0)
+            away(u)
+            step(0, 0)
+        else:
+            lax.fori_loop(0, 2, step, 0)
 
     copies = []
+
+    def away(u):
+        send(hbuf.at[u, 1], hidden_cols(core, u), h_s.at[u], h_r.at[u], partner)
 
     def hidden_cols(c, u):
         return hidden.at[:, lanes_at(c, u, 1)]
@@ -350,7 +363,8 @@
         c = pltpu.make_async_copy(hbuf.at[u, 0], hidden_cols(core, u), h_l.at[u])
         c.start()
         copies.append(c)
-        send(hbuf.at[u, 1], hidden_cols(core, u), h_s.at[u], h_r.at[u], partner)
+        if u != last:
+            away(u)
 
     does = {
         "rs": do_rs, "rs2": do_rs2, "upd": do_upd, "dd": do_dd, "st": do_st, "fw": do_fw, "fi": do_fi,
@@ -389,7 +403,7 @@
         c.wait()
 
 
-def held(a):
+def in_hbm(a):
     return pltpu.with_memory_space_constraint(a, pltpu.HBM)
 
 
@@ -412,8 +426,7 @@
             vmem((UNITS, 2, 4, 2, 4, 2, 16, 2 * LANES), bf16),
             vmem((2, 512, 2048), bf16),
             vmem((1024, 2048), bf16),
-            vmem((4, 16, 4096), bf16),
-            vmem((2, 16, 4096), bf16),
+            vmem((2, 4, 2, 16, 4096), bf16),
             vmem((4, 16, 4096), bf16),
             vmem((3, 16, 4096), bf16),
             vmem((3, 2, 16, 4096), bf16),
@@ -440,11 +453,11 @@
         ),
         name="outer_round",
     )(
-        held(tokens),
-        held(norm_gain.reshape(1, 2048)),
-        held(outer_params.reshape(2, 8, 16, 4096)),
-        held(momentum.reshape(2, 8, 16, 4096)),
-        held(deltas.reshape(2, 4, 2, 16, 4096)),
+        in_hbm(tokens),
+        in_hbm(norm_gain.reshape(1, 2048)),
+        in_hbm(outer_params.reshape(2, 8, 16, 4096)),
+        in_hbm(momentum.reshape(2, 8, 16, 4096)),
+        in_hbm(deltas.reshape(2, 4, 2, 16, 4096)),
     )
     here = pl.BlockSpec(memory_space=pltpu.VMEM)
     state = jax.ShapeDtypeStruct((2, 128, 4096), f32)

time: 110 us -> 109 us (level)
  no operation moved by 1% of the time
where the time goes in v5:
time: 109 us
  Pallas kernels  109 us (100%)
    pallas_call x1, Pallas kernels, body(): pl.pallas_call(kernel, out_shape=(jax.ShapeDtypeStruct((512, 4096), bf16)...  104 us
    pallas_call x1, Pallas kernels, body(): pl.pallas_call(finish, out_shape=(state, state, jax.ShapeDtypeStruct((512...  4.94 us

profile of v5, /device:TPU:1, one launch (start us, length us, event | category | flops | bytes accessed | tf_op | source)
XLA Modules:
  0.0 109.4 jit_solution(5420321971940325649)
XLA Ops:
  0.6 0.0 copy-start
  0.6 0.0 copy-start.1
  0.7 103.6 %outer_round.1 = (bf16[512,4096]{1,0:T(8,128)(2,1)S(1)}, bf16[2,4,2,16,4096]{4,3,2,1,0:T(8,128)(2,1)S(1)}) custom-call(bf16[512,2048]{1,0:T(8,128)(2,1)} %tokens.1, f32[1,2048]{1,0:T(1,128)} %bitcast.9, f32[2,8,16,4096]{3,2,1,0:T(8,128)} %bitcast.5, f32[2,8,16,4096]{3,2,1,0:T(8,128)} %bitcast.6, bf16[2,4,2,16,4096]{4,3,2,1,0:T(8,128)(2,1)} %bitcast.8), custom_call_target="tpu_custom_call" | custom-call | tf_op jit(solution)/shard_map/outer_round/pallas_call | solution.py:416
  104.2 0.0 copy-done
  104.3 0.0 copy-done.1
  104.3 4.9 %finish.1 = (f32[2,128,4096]{2,1,0:T(8,128)}, f32[2,128,4096]{2,1,0:T(8,128)}, bf16[512,4096]{1,0:T(8,128)(2,1)}) custom-call(f32[2,128,4096]{2,1,0:T(8,128)S(1)} %copy-done, f32[2,128,4096]{2,1,0:T(8,128)S(1)} %copy-done.1, bf16[2,128,4096]{2,1,0:T(8,128)(2,1)S(1)} %bitcast.7, bf16[512,4096]{1,0:T(8,128)(2,1)S(1)} %get-tuple-element.6.rows), custom_call_target="tpu_custom_call" | custom-call | tf_op jit(solution)/shard_map/finish/pallas_call | solution.py:464
Async XLA Ops:
  0.6 103.6 %copy-start = (f32[2,128,4096]{2,1,0:T(8,128)S(1)}, f32[2,128,4096]{2,1,0:T(8,128)}, u32[]{:S(2)}) copy-start(f32[2,128,4096]{2,1,0:T(8,128)} %params.1) | copy-start | bytes 12582916
  0.6 103.6 %copy-start.1 = (f32[2,128,4096]{2,1,0:T(8,128)S(1)}, f32[2,128,4096]{2,1,0:T(8,128)}, u32[]{:S(2)}) copy-start(f32[2,128,4096]{2,1,0:T(8,128)} %moment.1) | copy-start | bytes 12582916

commit v6 on v5

--- a/solution.py
+++ b/solution.py
@@ -17,57 +17,56 @@
 HALF = 2048
 
 ORDERS = {'x': ('y', 'z', 'x'), 'y': ('z', 'x', 'y'), 'z': ('x', 'y', 'z'), 'g': ('z', 'z', 'z', 'z')}
-SPANS = ((0, 3), (3, 4), (7, 3), (10, 3), (13, 3))
+SPANS = ((0, 4), (4, 5), (9, 4), (13, 3))
 PIECES = 2
-NORMS = 2
-SKEWED = (2, 7, 8, 10, 11, 13)
+NORMS = 4
+SKEWED = (0, 6, 8, 9)
 PLAN = (
     ('rs', 0), ('rs', 1), ('rs2', 0), ('rs', 2),
-    ('norm', 0), ('rs2', 1), ('rs', 3), ('norm', 1),
-    ('upd', 0), ('st', 0, 'z', 2, 1), ('st', 0, 'x', 0, 1), ('st', 0, 'y', 1, 1),
-    ('rs2', 2), ('rs', 4), ('dd', 0), ('upd', 1),
-    ('st', 0, 'z', 5, 2), ('st', 0, 'x', 3, 1), ('st', 0, 'y', 4, 1), ('fi', 0, 'z', 2, 1),
-    ('st', 1, 'z', 2, 1), ('fi', 0, 'x', 0, 1), ('st', 1, 'x', 0, 1), ('rs2', 3),
-    ('fi', 0, 'y', 1, 1), ('st', 1, 'y', 1, 1), ('dd', 1), ('upd', 2),
-    ('st', 0, 'z', 9, 1), ('st', 0, 'x', 7, 1), ('st', 0, 'y', 8, 1), ('fi', 0, 'z', 5, 2),
-    ('st', 1, 'z', 5, 1), ('st', 1, 'z', 6, 1), ('fi', 0, 'x', 3, 1), ('st', 1, 'x', 3, 1),
-    ('rs2', 4), ('fi', 0, 'y', 4, 1), ('st', 1, 'y', 4, 1), ('dd', 2),
-    ('fw', 1, 'y', 1, 1), ('fw', 1, 'z', 2, 1), ('fw', 1, 'x', 0, 1), ('fi', 0, 'x', 7, 1),
-    ('st', 1, 'x', 7, 1), ('fi', 0, 'z', 9, 1), ('st', 1, 'z', 9, 1), ('upd', 3),
-    ('st', 0, 'x', 10, 2), ('st', 0, 'y', 12, 1), ('fi', 0, 'y', 8, 1), ('st', 1, 'y', 8, 1),
-    ('fw', 1, 'z', 5, 1), ('fw', 1, 'x', 3, 1), ('fw', 1, 'y', 4, 1), ('fw', 1, 'z', 6, 1),
-    ('fi', 1, 'y', 1, 1), ('st', 2, 'y', 1, 1), ('dd', 3), ('fi', 1, 'x', 0, 1),
-    ('st', 2, 'x', 0, 1), ('fi', 1, 'z', 2, 1), ('st', 2, 'z', 2, 1), ('upd', 4),
-    ('fw', 1, 'y', 8, 1), ('fi', 1, 'y', 4, 1), ('st', 0, 'y', 14, 2), ('fi', 1, 'x', 3, 1),
-    ('st', 2, 'x', 3, 1), ('st', 0, 'x', 13, 1), ('fi', 0, 'y', 12, 1), ('dd', 4),
-    ('fi', 1, 'z', 5, 1), ('fw', 1, 'z', 9, 1), ('fw', 1, 'x', 7, 1), ('fi', 0, 'x', 10, 2),
-    ('st', 2, 'y', 4, 1), ('st', 1, 'x', 10, 1), ('fi', 1, 'z', 6, 1), ('st', 1, 'y', 12, 1),
-    ('st', 1, 'x', 11, 1), ('st', 2, 'z', 5, 1), ('fi', 1, 'y', 8, 1), ('fw', 2, 'x', 0, 1),
-    ('fw', 2, 'y', 1, 1), ('fi', 1, 'x', 7, 1), ('fi', 0, 'y', 14, 2), ('fi', 1, 'z', 9, 1),
-    ('fi', 0, 'x', 13, 1), ('st', 1, 'y', 14, 1), ('st', 1, 'y', 15, 1), ('st', 2, 'y', 8, 1),
-    ('fw', 1, 'x', 10, 1), ('fw', 1, 'x', 11, 1), ('st', 1, 'x', 13, 1), ('fw', 1, 'y', 12, 1),
-    ('fw', 2, 'x', 3, 1), ('fw', 2, 'z', 2, 1), ('fi', 2, 'x', 0, 1), ('st', 2, 'x', 7, 1),
-    ('fw', 2, 'y', 4, 1), ('st', 2, 'z', 6, 1), ('mm', 0), ('em', 0),
-    ('gy0',), ('fi', 1, 'x', 10, 1), ('fi', 1, 'x', 11, 1), ('fi', 2, 'y', 1, 1),
-    ('fi', 1, 'y', 12, 1), ('st', 2, 'y', 12, 1), ('mm', 1), ('em', 1),
-    ('fw', 1, 'x', 13, 1), ('fi', 2, 'z', 2, 1), ('fw', 1, 'y', 14, 1), ('fw', 1, 'y', 15, 1),
-    ('fw', 2, 'z', 5, 1), ('fi', 2, 'x', 3, 1), ('st', 2, 'x', 10, 1), ('mm', 2),
-    ('em', 2), ('mm', 3), ('em', 3), ('fw', 2, 'y', 8, 1),
-    ('st', 2, 'z', 9, 1), ('fi', 2, 'y', 4, 1), ('mm', 4), ('em', 4),
-    ('fi', 1, 'x', 13, 1), ('fw', 2, 'x', 7, 1), ('fi', 1, 'y', 14, 1), ('fi', 1, 'y', 15, 1),
-    ('st', 2, 'y', 14, 1), ('gy1',), ('fw', 2, 'z', 6, 1), ('fi', 2, 'z', 5, 1),
-    ('st', 2, 'x', 11, 1), ('mm', 5), ('em', 5), ('st', 2, 'y', 15, 1),
-    ('st', 3, 'g', 0, 1), ('fi', 2, 'y', 8, 1), ('fw', 2, 'x', 10, 1), ('mm', 8),
-    ('em', 8), ('fi', 2, 'x', 7, 1), ('fw', 2, 'z', 9, 1), ('mm', 7),
-    ('em', 7), ('st', 2, 'x', 13, 1), ('fi', 2, 'z', 6, 1), ('mm', 6),
-    ('em', 6), ('fw', 2, 'y', 12, 1), ('st', 3, 'g', 1, 1), ('fw', 2, 'y', 14, 1),
-    ('fw', 2, 'x', 11, 1), ('fi', 2, 'x', 10, 1), ('mm', 10), ('em', 10),
-    ('fw', 3, 'g', 0, 1), ('fw', 2, 'y', 15, 1), ('fi', 2, 'z', 9, 1), ('mm', 9),
-    ('em', 9), ('fi', 2, 'y', 12, 1), ('mm', 12), ('em', 12),
-    ('fw', 2, 'x', 13, 1), ('fi', 2, 'y', 14, 1), ('fw', 3, 'g', 1, 1), ('mm', 14),
-    ('em', 14), ('fi', 2, 'x', 11, 1), ('mm', 11), ('em', 11),
-    ('fi', 2, 'y', 15, 1), ('fi', 3, 'g', 0, 1), ('mm', 15), ('em', 15),
-    ('fi', 2, 'x', 13, 1), ('mm', 13), ('em', 13), ('fi', 3, 'g', 1, 1),
+    ('norm', 0), ('norm', 1), ('norm', 2), ('rs2', 1),
+    ('rs', 3), ('norm', 3), ('upd', 0), ('st', 0, 'z', 2, 2),
+    ('st', 0, 'x', 0, 1), ('dd', 0), ('st', 0, 'y', 1, 1), ('rs2', 2),
+    ('upd', 1), ('st', 0, 'z', 8, 1), ('st', 0, 'x', 4, 2), ('st', 0, 'y', 6, 2),
+    ('fi', 0, 'x', 0, 1), ('st', 1, 'x', 0, 1), ('fi', 0, 'z', 2, 2), ('st', 1, 'z', 2, 1),
+    ('rs2', 3), ('st', 1, 'z', 3, 1), ('fi', 0, 'y', 1, 1), ('st', 1, 'y', 1, 1),
+    ('dd', 1), ('upd', 2), ('st', 0, 'z', 12, 1), ('st', 0, 'x', 9, 2),
+    ('st', 0, 'y', 11, 1), ('fi', 0, 'z', 8, 1), ('st', 1, 'z', 8, 1), ('fi', 0, 'y', 6, 2),
+    ('st', 1, 'y', 6, 1), ('st', 1, 'y', 7, 1), ('fi', 0, 'x', 4, 2), ('st', 1, 'x', 4, 1),
+    ('st', 1, 'x', 5, 1), ('fw', 1, 'z', 2, 1), ('dd', 2), ('fw', 1, 'y', 1, 1),
+    ('fw', 1, 'z', 3, 1), ('fw', 1, 'x', 0, 1), ('upd', 3), ('st', 0, 'x', 13, 1),
+    ('gy0',), ('st', 0, 'y', 14, 2), ('fi', 0, 'y', 11, 1), ('st', 1, 'y', 11, 1),
+    ('fi', 0, 'z', 12, 1), ('st', 1, 'z', 12, 1), ('fw', 1, 'y', 6, 1), ('fw', 1, 'x', 4, 1),
+    ('fi', 0, 'x', 9, 2), ('st', 1, 'x', 9, 1), ('dd', 3), ('fw', 1, 'z', 8, 1),
+    ('fw', 1, 'y', 7, 1), ('st', 1, 'x', 10, 1), ('fi', 1, 'z', 2, 1), ('fi', 1, 'y', 1, 1),
+    ('st', 2, 'y', 1, 1), ('fi', 1, 'z', 3, 1), ('fi', 1, 'x', 0, 1), ('st', 2, 'x', 0, 1),
+    ('fw', 1, 'x', 5, 1), ('st', 2, 'z', 2, 1), ('fi', 0, 'x', 13, 1), ('fi', 1, 'y', 6, 1),
+    ('fi', 1, 'x', 4, 1), ('fi', 0, 'y', 14, 2), ('fi', 1, 'y', 7, 1), ('fi', 1, 'z', 8, 1),
+    ('fw', 1, 'y', 11, 1), ('st', 2, 'y', 6, 1), ('fi', 1, 'x', 5, 1), ('st', 1, 'y', 14, 1),
+    ('gy1',), ('st', 1, 'y', 15, 1), ('fw', 1, 'x', 9, 1), ('fw', 1, 'x', 10, 1),
+    ('fw', 2, 'x', 0, 1), ('st', 2, 'z', 3, 1), ('fi', 1, 'y', 11, 1), ('fw', 1, 'y', 14, 1),
+    ('fw', 1, 'z', 12, 1), ('st', 2, 'y', 7, 1), ('fi', 1, 'x', 9, 1), ('st', 2, 'x', 4, 1),
+    ('fi', 1, 'x', 10, 1), ('fi', 2, 'x', 0, 1), ('fw', 2, 'z', 2, 1), ('mm', 0),
+    ('em', 0), ('fw', 2, 'y', 1, 1), ('fi', 1, 'y', 14, 1), ('fw', 1, 'y', 15, 1),
+    ('st', 2, 'x', 5, 1), ('fw', 2, 'z', 3, 1), ('fi', 1, 'z', 12, 1), ('fw', 2, 'y', 6, 1),
+    ('st', 2, 'z', 8, 1), ('fi', 2, 'z', 2, 1), ('mm', 2), ('em', 2),
+    ('fi', 1, 'y', 15, 1), ('fi', 2, 'z', 3, 1), ('fw', 2, 'x', 4, 1), ('st', 2, 'y', 11, 1),
+    ('mm', 3), ('em', 3), ('st', 1, 'x', 13, 1), ('fw', 2, 'x', 5, 1),
+    ('st', 2, 'z', 12, 1), ('fi', 2, 'y', 1, 1), ('mm', 1), ('em', 1),
+    ('st', 2, 'x', 9, 1), ('fw', 2, 'y', 7, 1), ('fi', 2, 'y', 6, 1), ('mm', 6),
+    ('em', 6), ('fi', 2, 'x', 4, 1), ('mm', 4), ('em', 4),
+    ('st', 2, 'y', 14, 1), ('fw', 2, 'z', 8, 1), ('fi', 2, 'x', 5, 1), ('mm', 5),
+    ('em', 5), ('st', 2, 'x', 10, 1), ('fw', 1, 'x', 13, 1), ('fw', 2, 'z', 12, 1),
+    ('fi', 2, 'y', 7, 1), ('mm', 7), ('em', 7), ('fw', 2, 'y', 11, 1),
+    ('st', 3, 'g', 0, 1), ('fi', 2, 'z', 8, 1), ('mm', 8), ('em', 8),
+    ('fw', 2, 'x', 9, 1), ('st', 2, 'y', 15, 1), ('fi', 1, 'x', 13, 1), ('st', 2, 'x', 13, 1),
+    ('fi', 2, 'z', 12, 1), ('mm', 12), ('em', 12), ('st', 3, 'g', 1, 1),
+    ('fi', 2, 'y', 11, 1), ('mm', 11), ('em', 11), ('fw', 2, 'y', 14, 1),
+    ('fi', 2, 'x', 9, 1), ('mm', 9), ('em', 9), ('fw', 2, 'x', 10, 1),
+    ('fw', 2, 'y', 15, 1), ('fw', 3, 'g', 0, 1), ('fw', 2, 'x', 13, 1), ('fi', 2, 'y', 14, 1),
+    ('fw', 3, 'g', 1, 1), ('mm', 14), ('em', 14), ('fi', 2, 'x', 10, 1),
+    ('mm', 10), ('em', 10), ('fi', 3, 'g', 0, 1), ('fi', 2, 'y', 15, 1),
+    ('mm', 15), ('em', 15), ('fi', 2, 'x', 13, 1), ('mm', 13),
+    ('em', 13), ('fi', 3, 'g', 1, 1),
 )
 
 
@@ -332,8 +331,6 @@
 
     factor = 1.0 / math.sqrt(2048)
 
-    last = [op[1] for op in PLAN if op[0] == "mm"][-1]
-
     def do_mm(u):
         def step(m, carry):
             rows = pl.ds(pl.multiple_of(m * 512, 512), 512)
@@ -344,12 +341,7 @@
             hbuf[u, m] = ((gate / (1.0 + jnp.exp(-gate))) * up).astype(bf16)
             return carry
 
-        if u == last:
-            step(1, 0)
-            away(u)
-            step(0, 0)
-        else:
-            lax.fori_loop(0, 2, step, 0)
+        lax.fori_loop(0, 2, step, 0)
 
     copies = []
 
@@ -363,8 +355,7 @@
         c = pltpu.make_async_copy(hbuf.at[u, 0], hidden_cols(core, u), h_l.at[u])
         c.start()
         copies.append(c)
-        if u != last:
-            away(u)
+        away(u)
 
     does = {
         "rs": do_rs, "rs2": do_rs2, "upd": do_upd, "dd": do_dd, "st": do_st, "fw": do_fw, "fi": do_fi,

time: 109 us -> 109 us (level)
  no operation moved by 1% of the time
where the time goes in v6:
time: 109 us
  Pallas kernels  109 us (100%)
    pallas_call x1, Pallas kernels, body(): pl.pallas_call(kernel, out_shape=(jax.ShapeDtypeStruct((512, 4096), bf16)...  104 us
    pallas_call x1, Pallas kernels, body(): pl.pallas_call(finish, out_shape=(state, state, jax.ShapeDtypeStruct((512...  4.94 us

profile of v6, /device:TPU:1, one launch (start us, length us, event | category | flops | bytes accessed | tf_op | source)
XLA Modules:
  0.0 109.4 jit_solution(7176896686434155426)
XLA Ops:
  0.6 0.0 copy-start
  0.6 0.0 copy-start.1
  0.7 103.6 %outer_round.1 = (bf16[512,4096]{1,0:T(8,128)(2,1)S(1)}, bf16[2,4,2,16,4096]{4,3,2,1,0:T(8,128)(2,1)S(1)}) custom-call(bf16[512,2048]{1,0:T(8,128)(2,1)} %tokens.1, f32[1,2048]{1,0:T(1,128)} %bitcast.9, f32[2,8,16,4096]{3,2,1,0:T(8,128)} %bitcast.5, f32[2,8,16,4096]{3,2,1,0:T(8,128)} %bitcast.6, bf16[2,4,2,16,4096]{4,3,2,1,0:T(8,128)(2,1)} %bitcast.8), custom_call_target="tpu_custom_call" | custom-call | tf_op jit(solution)/shard_map/outer_round/pallas_call | solution.py:407
  104.3 0.0 copy-done
  104.3 0.0 copy-done.1
  104.3 4.9 %finish.1 = (f32[2,128,4096]{2,1,0:T(8,128)}, f32[2,128,4096]{2,1,0:T(8,128)}, bf16[512,4096]{1,0:T(8,128)(2,1)}) custom-call(f32[2,128,4096]{2,1,0:T(8,128)S(1)} %copy-done, f32[2,128,4096]{2,1,0:T(8,128)S(1)} %copy-done.1, bf16[2,128,4096]{2,1,0:T(8,128)(2,1)S(1)} %bitcast.7, bf16[512,4096]{1,0:T(8,128)(2,1)S(1)} %get-tuple-element.6.rows), custom_call_target="tpu_custom_call" | custom-call | tf_op jit(solution)/shard_map/finish/pallas_call | solution.py:455
Async XLA Ops:
  0.6 103.6 %copy-start = (f32[2,128,4096]{2,1,0:T(8,128)S(1)}, f32[2,128,4096]{2,1,0:T(8,128)}, u32[]{:S(2)}) copy-start(f32[2,128,4096]{2,1,0:T(8,128)} %params.1) | copy-start | bytes 12582916
  0.6 103.6 %copy-start.1 = (f32[2,128,4096]{2,1,0:T(8,128)S(1)}, f32[2,128,4096]{2,1,0:T(8,128)}, u32[]{:S(2)}) copy-start(f32[2,128,4096]{2,1,0:T(8,128)} %moment.1) | copy-start | bytes 12582916
